TPU v7x, 256 devices: a 8x8x2 block of a 8x8x16 slice. The times are simulated.
256 devices in a mesh: clips: 2 (over z), tm: 16 (over y, core), height: 8 (over x).
Axes of the slice: x: 8, y: 8, z: 2, core: 2. Of those that a mesh axis runs over, the one named last changes fastest.
The devices are a block of a 8x8x16 slice.
Arguments:
- features: bfloat16 [64, 32, 96, 512], P(('clips', 'tm'), 'height'), parts along dimension 0, may hold values from -1000 to 1000
- gain: float32 [512], replicated, may hold values from 0.1 to 1.9
- shift: float32 [512], replicated, may hold values from -3 to 3
- kernel: bfloat16 [3, 3, 3, 512, 256], replicated, may hold values from -0.0546875 to 0.0546875
- bias: float32 [256], replicated, may hold values from -3 to 3
Outputs:
- decoded: bfloat16 [64, 32, 96, 256], P(('clips', 'tm'), 'height'), parts along dimension 0
There are 2 independent parts, one for each index of `clips`. A program takes and returns all parts, laid end to end along the dimension named above; an argument that names none is the same for every part. Nothing has to cross between parts.
All inputs are finite; a program needn't handle non-finite values.
Results may differ from a plain program's by a relative error of at most 0.0055.
Values may be sent and summed in bfloat16 or wider, within the bound.
A program may use at most 64 MiB of HBM per device.

v0:
```python
import jax
import jax.numpy as jnp
from jax import lax
from jax.sharding import Mesh
from jax.sharding import PartitionSpec as P

GROUPS = 32
TM = ("tm_0", "tm_1")
TM_HEIGHT = ("tm_0", "tm_1", "height")
CLIPS_TM = ("clips", "tm_0", "tm_1")


epsilon = 1e-06


def by_axis(shard, axes):
    for axis in axes:
        shard = lax.psum(shard, axis)
    return shard


def passed_along(value, axis, steps):
    count = lax.axis_size(axis)
    initial, last = (max(0, -steps), min(count, count - steps))
    return lax.ppermute(value, axis, [(source, source + steps) for source in range(initial, last)])


def padded(block, sides, width):
    for axis, dim in sides:
        count = lax.axis_size(axis)
        forward = [(i, i + 1) for i in range(count - 1)]
        backward = [(target, source) for source, target in forward]
        low = lax.ppermute(
            lax.slice_in_dim(block, block.shape[dim] - width, None, axis=dim), axis, forward
        )
        high = lax.ppermute(lax.slice_in_dim(block, 0, width, axis=dim), axis, backward)
        block = jnp.concatenate([low, block, high], axis=dim)
    return block


def spatial(frames, kernel_plane):
    count_frames, padded_rows, padded_cols, channels = frames.shape
    inner_rows = padded_rows - 2
    inner_cols = padded_cols - 2
    summed = jnp.zeros(
        (count_frames * inner_rows * inner_cols, kernel_plane.shape[-1]), jnp.float32
    )
    for b in range(3):
        for c in range(3):
            window = frames[:, b : b + inner_rows, c : c + inner_cols, :].reshape(-1, channels)
            summed = summed + jnp.dot(
                window, kernel_plane[b, c], preferred_element_type=jnp.float32
            )
    return summed.reshape(count_frames, inner_rows, inner_cols, -1)


def pad_columns(frames):
    return jnp.pad(frames, ((0, 0), (0, 0), (1, 1), (0, 0)))


def on_device(features, gain, shift, kernel, bias):
    frames_dev, rows_dev, cols_dev, channels = features.shape
    per_group = channels // GROUPS
    wide_values = features.astype(jnp.float32).reshape(
        frames_dev, rows_dev, cols_dev, GROUPS, per_group
    )
    cells_total = (
        lax.axis_size(TM) * lax.axis_size("height") * frames_dev * rows_dev * cols_dev * per_group
    )
    local_sums = jnp.sum(wide_values, axis=(0, 1, 2, 4))
    squares = jnp.sum(wide_values * wide_values, axis=(0, 1, 2, 4))
    summed_all, squares_all = (by_axis(local_sums, TM_HEIGHT), by_axis(squares, TM_HEIGHT))
    group_mean = summed_all / cells_total
    group_var = squares_all / cells_total - group_mean * group_mean
    centered = wide_values - group_mean[:, None]
    normed = centered * lax.rsqrt(group_var + epsilon)[:, None]
    normed = normed.reshape(frames_dev, rows_dev, cols_dev, channels) * gain + shift
    activated = jax.nn.silu(normed).astype(jnp.bfloat16)
    tm_index = lax.axis_index(TM)
    first_pair = jnp.concatenate([activated[:1], activated[:1]], 0)
    earlier = passed_along(activated, TM, 1)
    earlier = jnp.where(tm_index == 0, first_pair, earlier)
    slab = jnp.concatenate([earlier, activated], 0)
    slab = pad_columns(padded(slab, (("height", 1),), 1))
    output = jnp.zeros((frames_dev, rows_dev, cols_dev, kernel.shape[-1]), jnp.float32)
    for a in range(3):
        output = output + spatial(slab[a : a + frames_dev], kernel[a])
    return (output + bias).astype(jnp.bfloat16)


def solution(mesh):
    torus = Mesh(
        mesh.devices.reshape(mesh.shape["clips"], 8, 2, mesh.shape["height"]),
        ("clips", "tm_0", "tm_1", "height"),
    )
    return jax.shard_map(
        on_device,
        mesh=torus,
        in_specs=(P(CLIPS_TM, "height", None, None), P(), P(), P(), P()),
        out_specs=P(CLIPS_TM, "height", None, None),
        check_vma=False,
    )
```

profile of v0, /device:TPU:528, one launch (start us, length us, event | category | flops | bytes accessed | tf_op | source)
XLA Modules:
  0.0 101.1 jit_solution(3148883409344995435)
XLA Ops:
  0.0 1.4 %convert_reduce_fusion = (f32[512]{0:T(512)S(1)}, f32[512]{0:T(512)S(1)}) fusion(bf16[2,4,96,512]{3,2,1,0:T(8,128)(2,1)} %param.5), kind=kLoop, calls=%fused_computation.10 | loop fusion | flops 1571840 | bytes 790528 | tf_op jit(solution)/shard_map/reduce_sum | solution.py:70
  1.4 0.1 reduce_sum.24
  1.5 0.1 reduce_sum.36
  1.5 0.1 reduce_sum.25
  1.7 0.1 reduce_sum.37
  1.8 32.4 %all-reduce.2 = (f32[32]{0:T(128)S(1)}, f32[32]{0:T(128)S(1)}) all-reduce(f32[32]{0:T(128)S(1)} %reduce_sum.37, f32[32]{0:T(128)S(1)} %reduce_sum.25), channel_id=1, replica_groups=mesh['clips'=2,'tm_0'=8,'tm_1'=2,'height'=8] {'tm_0'}, use_global_device_ids=true, to_apply=%region_7.0 | all-reduce | flops 64 | bytes 512 | tf_op jit(solution)/shard_map/psum | solution.py:18
  34.2 2.5 %all-reduce.3 = (f32[32]{0:T(128)S(1)}, f32[32]{0:T(128)S(1)}) all-reduce(f32[32]{0:T(128)S(1)} %get-tuple-element.9, f32[32]{0:T(128)S(1)} %get-tuple-element.10), channel_id=1, replica_groups=mesh['clips'=2,'tm_0'=8,'tm_1'=2,'height'=8] {'tm_1'}, use_global_device_ids=true, to_apply=%region_8.9 | all-reduce | flops 64 | bytes 512 | tf_op jit(solution)/shard_map/psum | solution.py:18
  36.7 14.2 %all-reduce.1 = (f32[32]{0:T(128)S(1)}, f32[32]{0:T(128)S(1)}) all-reduce(f32[32]{0:T(128)S(1)} %get-tuple-element.11, f32[32]{0:T(128)S(1)} %get-tuple-element.12), channel_id=1, replica_groups=mesh['clips'=2,'tm_0'=8,'tm_1'=2,'height'=8] {'height'}, use_global_device_ids=true, to_apply=%region_9.10 | all-reduce | flops 64 | bytes 512 | tf_op jit(solution)/shard_map/psum | solution.py:18
  50.9 0.1 mul.38
  51.0 0.1 mul.39
  51.1 0.1 sub.16
  51.2 0.1 sub.17
  51.2 1.7 %fusion.12 = bf16[2,4,96,512]{3,2,1,0:T(8,128)(2,1)S(1)} fusion(bf16[2,4,96,512]{3,2,1,0:T(8,128)(2,1)} %param.5, f32[512]{0:T(512)} %param.7, f32[512]{0:T(512)} %param.6, f32[512]{0:T(512)S(1)} %mul.39, f32[512]{0:T(512)S(1)} %sub.17), kind=kLoop, calls=%fused_computation.24 | loop fusion | flops 3932160 | bytes 1581056 | tf_op jit(solution)/shard_map/convert_element_type | solution.py:78
  52.9 2.0 %collective-permute-start = (bf16[2,4,96,512]{3,2,1,0:T(8,128)(2,1)S(1)}, bf16[2,4,96,512]{3,2,1,0:T(8,128)(2,1)S(1)}, u32[]{:S(2)}, u32[]{:S(2)}) collective-permute-start(bf16[2,4,96,512]{3,2,1,0:T(8,128)(2,1)S(1)} %fusion.12), channel_id=1, source_target_pairs={{0,8},{8,16},{16,24},{24,32},{32,40},{40,48},{48,56},{56,64},{64,7... | collective-permute-start | bytes 2359304 | tf_op jit(solution)/shard_map/ppermute | solution.py:25
  55.0 3.8 %slice_bitcast_fusion.2 = (bf16[3,3,512,256]{3,2,1,0:T(8,128)(2,1)S(1)}, bf16[3,3,512,256]{3,2,1,0:T(8,128)(2,1)S(1)}, bf16[3,3,512,256]{3,2,1,0:T(8,128)(2,1)S(1)}) fusion(bf16[3,3,3,512,256]{4,3,2,1,0:T(8,128)(2,1)} %param.8), kind=kLoop, calls=%fused_computation.13 | loop fusion | bytes 14155776 | tf_op jit(solution)/shard_map/squeeze | solution.py:87
  58.8 0.4 fusion.24
  59.2 7.1 %collective-permute-done = bf16[2,4,96,512]{3,2,1,0:T(8,128)(2,1)S(1)} collective-permute-done((bf16[2,4,96,512]{3,2,1,0:T(8,128)(2,1)S(1)}, bf16[2,4,96,512]{3,2,1,0:T(8,128)(2,1)S(1)}, u32[]{:S(2)}, u32[]{:S(2)}) %collective-permute-start) | collective-permute-done | bytes 786464 | tf_op jit(solution)/shard_map/ppermute | solution.py:25
  66.3 0.1 maximum_select_fusion
  66.4 0.1 pad_maximum_fusion.3
  66.5 0.1 pad_maximum_fusion.1
  66.6 3.9 %collective-permute-start.1 = (bf16[4,1,96,512]{3,2,1,0:T(8,128)(2,1)S(1)}, bf16[4,1,96,512]{3,2,1,0:T(8,128)(2,1)S(1)}, u32[]{:S(2)}, u32[]{:S(2)}) collective-permute-start(bf16[4,1,96,512]{3,2,1,0:T(8,128)(2,1)S(1)} %get-tuple-element.42), channel_id=1, source_target_pairs={{0,1},{1,2},{2,3},{3,4},{4,5},{5,6},{6,7},{8,9},{9,10},{10,11},{11... | collective-permute-start | bytes 1179656 | tf_op jit(solution)/shard_map/ppermute | solution.py:33
  70.5 1.5 %collective-permute-start.2 = (bf16[4,1,96,512]{3,2,1,0:T(8,128)(2,1)S(1)}, bf16[4,1,96,512]{3,2,1,0:T(8,128)(2,1)S(1)}, u32[]{:S(2)}, u32[]{:S(2)}) collective-permute-start(bf16[4,1,96,512]{3,2,1,0:T(8,128)(2,1)S(1)} %get-tuple-element.43), channel_id=1, source_target_pairs={{1,0},{2,1},{3,2},{4,3},{5,4},{6,5},{7,6},{9,8},{10,9},{11,10},{12... | collective-permute-start | bytes 1179656 | tf_op jit(solution)/shard_map/ppermute | solution.py:36
  72.0 1.2 %fusion.32 = f32[768,256]{1,0:T(8,128)} fusion(bf16[768,512]{1,0:T(8,128)(2,1)S(1)} %bitcast.169, bf16[3,3,512,256]{3,2,1,0:T(8,128)(2,1)S(1)} %get-tuple-element.15), kind=kOutput, calls=%fused_computation.65 | convolution fusion | flops 201326592 | bytes 1835008 | tf_op jit(solution)/shard_map/dot_general | solution.py:51
  73.2 0.4 fusion.41
  73.6 2.2 %collective-permute-done.1 = bf16[4,1,96,512]{3,2,1,0:T(8,128)(2,1)S(1)} collective-permute-done((bf16[4,1,96,512]{3,2,1,0:T(8,128)(2,1)S(1)}, bf16[4,1,96,512]{3,2,1,0:T(8,128)(2,1)S(1)}, u32[]{:S(2)}, u32[]{:S(2)}) %collective-permute-start.1) | collective-permute-done | bytes 393248 | tf_op jit(solution)/shard_map/ppermute | solution.py:33
  75.8 4.4 %collective-permute-done.2 = bf16[4,1,96,512]{3,2,1,0:T(8,128)(2,1)S(1)} collective-permute-done((bf16[4,1,96,512]{3,2,1,0:T(8,128)(2,1)S(1)}, bf16[4,1,96,512]{3,2,1,0:T(8,128)(2,1)S(1)}, u32[]{:S(2)}, u32[]{:S(2)}) %collective-permute-start.2) | collective-permute-done | bytes 393248 | tf_op jit(solution)/shard_map/ppermute | solution.py:36
  80.2 0.5 maximum_maximum_fusion
  80.7 1.5 %fusion.47 = (bf16[2,4,96,512]{3,2,1,0:T(8,128)(2,1)}, bf16[2,4,96,512]{3,2,1,0:T(8,128)(2,1)}, bf16[2,4,96,512]{3,2,1,0:T(8,128)(2,1)S(1)}, bf16[2,4,96,512]{3,...) fusion(bf16[4,5,96,512]{3,2,1,0:T(8,128)(2,1)S(1)} %get-tuple-element.40, ...), kind=kLoop, calls=%fused_computation.95 | loop fusion | bytes 9437184 | tf_op jit(solution)/shard_map/slice | solution.py:50
  82.2 1.3 %fusion.30 = f32[768,256]{1,0:T(8,128)} fusion(bf16[768,512]{1,0:T(8,128)(2,1)S(1)} %bitcast.168, bf16[3,3,512,256]{3,2,1,0:T(8,128)(2,1)S(1)} %get-tuple-element.15), kind=kOutput, calls=%fused_computation.60 | convolution fusion | flops 201326592 | bytes 1835008 | tf_op jit(solution)/shard_map/dot_general | solution.py:51
  83.5 1.3 %fusion.35 = f32[768,256]{1,0:T(8,128)} fusion(bf16[768,512]{1,0:T(8,128)(2,1)S(1)} %bitcast.167, bf16[3,3,512,256]{3,2,1,0:T(8,128)(2,1)S(1)} %get-tuple-element.15), kind=kOutput, calls=%fused_computation.71 | convolution fusion | flops 201326592 | bytes 1835008 | tf_op jit(solution)/shard_map/dot_general | solution.py:51
  84.7 1.5 %select_maximum_fusion = bf16[4,6,98,512]{3,2,1,0:T(8,128)(2,1)S(1)} fusion(bf16[4,1,96,512]{3,2,1,0:T(8,128)(2,1)S(1)} %collective-permute-done.2, bf16[4,1,96,512]{3,2,1,0:T(8,128)(2,1)S(1)} %collective-permute-done.1, bf16[2,4,96,512]{3,2,1,0:T(8,128)(2,1)S(1)} %fusion.12, bf16[2,4,96,512]{3,2,1,0:T(8,128)(2,1)S(1)} %maximum_select_fusion), kind=kLoop, calls=%fused_computation.3 | loop fusion | flops 18063360 | bytes 4767744 | tf_op jit(solution)/shard_map/concatenate | solution.py:37
  86.2 4.6 %fusion.46 = (bf16[2,4,96,512]{3,2,1,0:T(8,128)(2,1)S(1)}, bf16[2,4,96,512]{3,2,1,0:T(8,128)(2,1)S(1)}, bf16[2,4,96,512]{3,2,1,0:T(8,128)(2,1)S(1)}, bf16[2,4,96...) fusion(bf16[4,6,98,512]{3,2,1,0:T(8,128)(2,1)S(1)} %select_maxi, ...), kind=kLoop, calls=%fused_computation.94 | loop fusion | bytes 28311552 | tf_op jit(solution)/shard_map/slice | solution.py:50
  90.9 0.4 fusion.29
  91.2 0.4 fusion.31
  91.6 0.4 fusion.33
  92.0 0.4 fusion.34
  92.4 0.4 fusion.36
  92.8 0.4 fusion.38
  93.1 0.1 copy-done.1
  93.2 0.4 fusion.44
  93.6 0.1 copy-done
  93.6 0.4 fusion.27
  94.0 0.4 fusion.22
  94.4 0.4 fusion.21
  94.7 0.4 fusion.23
  95.1 0.4 fusion.25
  95.5 0.4 fusion.26
  95.8 0.4 fusion.28
  96.2 0.4 fusion.37
  96.6 0.4 fusion.39
  97.0 0.4 fusion.40
  97.3 0.0 copy-start.3
  97.3 0.0 copy-start.4
  97.4 0.0 copy-start.5
  97.4 0.4 fusion.42
  97.7 0.4 fusion.43
  98.1 0.4 fusion.45
  98.5 0.2 copy-done.4
  98.7 0.2 copy-done.5
  98.9 0.4 fusion.20
  99.4 0.0 copy-start.6
  99.4 0.9 fusion.17
  100.3 0.0 copy-done.6
  100.3 0.8 add_convert_fusion
  (7 shorter events, 0.0 us)
Async XLA Ops:
  52.9 13.3 %collective-permute-start = (bf16[2,4,96,512]{3,2,1,0:T(8,128)(2,1)S(1)}, bf16[2,4,96,512]{3,2,1,0:T(8,128)(2,1)S(1)}, u32[]{:S(2)}, u32[]{:S(2)}) collective-permute-start(bf16[2,4,96,512]{3,2,1,0:T(8,128)(2,1)S(1)} %fusion.12), channel_id=1, source_target_pairs={{0,8},{8,16},{16,24},{24,32},{32,40},{40,48},{48,56},{56,64},{64,7... | collective-permute-start | bytes 2359304 | tf_op jit(solution)/shard_map/ppermute | solution.py:25
  66.6 9.2 %collective-permute-start.1 = (bf16[4,1,96,512]{3,2,1,0:T(8,128)(2,1)S(1)}, bf16[4,1,96,512]{3,2,1,0:T(8,128)(2,1)S(1)}, u32[]{:S(2)}, u32[]{:S(2)}) collective-permute-start(bf16[4,1,96,512]{3,2,1,0:T(8,128)(2,1)S(1)} %get-tuple-element.42), channel_id=1, source_target_pairs={{0,1},{1,2},{2,3},{3,4},{4,5},{5,6},{6,7},{8,9},{9,10},{10,11},{11... | collective-permute-start | bytes 1179656 | tf_op jit(solution)/shard_map/ppermute | solution.py:33
  70.5 9.7 %collective-permute-start.2 = (bf16[4,1,96,512]{3,2,1,0:T(8,128)(2,1)S(1)}, bf16[4,1,96,512]{3,2,1,0:T(8,128)(2,1)S(1)}, u32[]{:S(2)}, u32[]{:S(2)}) collective-permute-start(bf16[4,1,96,512]{3,2,1,0:T(8,128)(2,1)S(1)} %get-tuple-element.43), channel_id=1, source_target_pairs={{1,0},{2,1},{3,2},{4,3},{5,4},{6,5},{7,6},{9,8},{10,9},{11,10},{12... | collective-permute-start | bytes 1179656 | tf_op jit(solution)/shard_map/ppermute | solution.py:36
  91.6 1.1 %copy-start.2 = (bf16[2,4,96,512]{3,2,1,0:T(8,128)(2,1)S(1)}, bf16[2,4,96,512]{3,2,1,0:T(8,128)(2,1)}, u32[]{:S(2)}) copy-start(bf16[2,4,96,512]{3,2,1,0:T(8,128)(2,1)} %get-tuple-element.48) | copy-start | bytes 2359300
  92.0 1.2 %copy-start.1 = (bf16[2,4,96,512]{3,2,1,0:T(8,128)(2,1)S(1)}, bf16[2,4,96,512]{3,2,1,0:T(8,128)(2,1)}, u32[]{:S(2)}) copy-start(bf16[2,4,96,512]{3,2,1,0:T(8,128)(2,1)} %get-tuple-element.34) | copy-start | bytes 2359300
  92.4 1.3 %copy-start = (bf16[2,4,96,512]{3,2,1,0:T(8,128)(2,1)S(1)}, bf16[2,4,96,512]{3,2,1,0:T(8,128)(2,1)}, u32[]{:S(2)}) copy-start(bf16[2,4,96,512]{3,2,1,0:T(8,128)(2,1)} %get-tuple-element.35) | copy-start | bytes 2359300
  97.3 1.1 %copy-start.3 = (f32[768,256]{1,0:T(8,128)S(1)}, f32[768,256]{1,0:T(8,128)}, u32[]{:S(2)}) copy-start(f32[768,256]{1,0:T(8,128)} %fusion.32) | copy-start | bytes 2359300
  97.3 1.4 %copy-start.4 = (f32[768,256]{1,0:T(8,128)S(1)}, f32[768,256]{1,0:T(8,128)}, u32[]{:S(2)}) copy-start(f32[768,256]{1,0:T(8,128)} %fusion.30) | copy-start | bytes 2359300
  97.4 1.6 %copy-start.5 = (f32[768,256]{1,0:T(8,128)S(1)}, f32[768,256]{1,0:T(8,128)}, u32[]{:S(2)}) copy-start(f32[768,256]{1,0:T(8,128)} %fusion.35) | copy-start | bytes 2359300
  99.4 0.9 copy-start.6
where the time goes:
time: 101 us
  blocking collectives  49.1 us (49%)
  waiting for transfers between devices  13.7 us (14%)
  matrix products  13.1 us (13%)
  local copies, waits for them, and re-layouts  11.1 us (11%)
  starting transfers between devices  7.38 us (7%)
  other arithmetic  6.37 us (6%)
    psum x3, blocking collectives, by_axis(): shard = lax.psum(shard, axis)  49.1 us
    dot_general x27, matrix products, spatial(): jnp.dot(window, kernel_plane[b, c], preferred_element_type=jnp.float32)  13.1 us
    ppermute x1, waiting for transfers between devices, passed_along(): lax.ppermute(value, axis, [(source, source + steps) for source in range(i...  7.11 us
    slice x2, local copies, waits for them, and re-layouts, spatial(): frames[:, b:b + inner_rows, c:c + inner_cols, :].reshape(-1, channels)  6.15 us
    ppermute x1, waiting for transfers between devices, padded(): lax.ppermute(lax.slice_in_dim(block, 0, width, axis=dim), axis, backward)  4.45 us
    ppermute x1, starting transfers between devices, padded(): lax.ppermute(lax.slice_in_dim(block, block.shape[dim] - width, None, axis...  3.94 us
    squeeze x1, local copies, waits for them, and re-layouts, on_device(): output = output + spatial(slab[a:a + frames_dev], kernel[a])  3.84 us
    ppermute x1, waiting for transfers between devices, padded(): lax.ppermute(lax.slice_in_dim(block, block.shape[dim] - width, None, axis...  2.15 us
  transfers between devices with their start and end apart: 3, of which 3 were waited for; matrix products, arithmetic and copies ran while one was open for 6% of the time, Pallas kernels for 0%

commit v1 on v0

v1 whole, which is shorter than its diff:
```python
import functools

import jax
import jax.numpy as jnp
from jax import lax
from jax.experimental import pallas as pl
from jax.experimental.pallas import tpu as pltpu
from jax.sharding import PartitionSpec as P

MESH = pl.DeviceIdType.MESH
GROUPS = 32
EPSILON = 1e-06


def offsets(count):
    every = [d if d <= count // 2 else d - count for d in range(1, count)]
    return sorted(every, key=lambda d: -abs(d))


def kernel(sizes, feat, gain, shift, weight, bias, out, raw, act, wbuf, obuf, gbuf, hbuf, bbuf,
           mine, row, got1, got2, in_sem, small_sem, w_sem, out_sem, s1, r1, s2, r2, hs, hr):
    tm_n, h_n = sizes
    y_n = tm_n // 2
    frames, rows, cols, channels = feat.shape
    lanes = 128
    parts = channels // lanes
    tm = lax.axis_index("tm")
    h = lax.axis_index("height")
    core = lax.rem(tm, 2)
    y = lax.div(tm, 2)
    first, last = tm == 0, tm == tm_n - 1
    top, bottom = h == 0, h == h_n - 1

    def turned(v, d, n):
        return lax.rem(v + (d + n), n)

    def near(dtm, dh):
        return {"tm": turned(tm, dtm, tm_n), "height": turned(h, dh, h_n)}

    def plane(dy, dc, dh):
        c = core if dc == 0 else 1 - core
        return {"tm": turned(y, dy, y_n) * 2 + c, "height": turned(h, dh, h_n)}

    peers1 = [(0, 1, dh) for dh in offsets(h_n)] + [(0, 0, dh) for dh in offsets(h_n)]
    peers1 = sorted(peers1 + [(0, 1, 0)], key=lambda p: -abs(p[2]))
    peers2 = [(dy, 0, 0) for dy in offsets(y_n)]
    halo = [(1, 0), (-1, 0), (1, 1), (-1, 1), (1, -1), (-1, -1)]

    own = pltpu.make_async_copy(feat, raw.at[frames:, 1 : 1 + rows], in_sem)
    own.start()
    smalls = [pltpu.make_async_copy(a, b, small_sem.at[i])
              for i, (a, b) in enumerate(((gain, gbuf), (shift, hbuf), (bias, bbuf)))]
    for copy in smalls:
        copy.start()
    weights = pltpu.make_async_copy(weight, wbuf, w_sem)
    weights.start()

    barrier = pltpu.get_barrier_semaphore()
    for p in peers1 + peers2:
        pl.semaphore_signal(barrier, inc=1, device_id=plane(*p), device_id_type=MESH)
    for p in halo:
        pl.semaphore_signal(barrier, inc=1, device_id=near(*p), device_id_type=MESH)

    own.wait()
    total = jnp.zeros((8, channels), jnp.float32)
    squares = jnp.zeros((8, channels), jnp.float32)
    for f in range(frames):
        for r in range(rows):
            x = raw[frames + f, 1 + r].astype(jnp.float32).reshape(cols // 8, 8, channels)
            total = total + jnp.sum(x, axis=0)
            squares = squares + jnp.sum(x * x, axis=0)
    total = jnp.sum(total, axis=0, keepdims=True)
    squares = jnp.sum(squares, axis=0, keepdims=True)
    for k in range(parts):
        mine[k : k + 1, :] = total[:, k * lanes : (k + 1) * lanes]
        mine[parts + k : parts + k + 1, :] = squares[:, k * lanes : (k + 1) * lanes]

    pl.semaphore_wait(barrier, len(peers1) + len(peers2) + len(halo))

    def send(src, dst, s, r, device):
        return pltpu.make_async_remote_copy(src_ref=src, dst_ref=dst, send_sem=s, recv_sem=r,
                                            device_id=device, device_id_type=MESH)

    for i, p in enumerate(peers1):
        send(mine, got1.at[i], s1, r1, plane(*p)).start()

    def edge(src_row, dst_row, frame, dtm, dh, i):
        return send(raw.at[frames:, src_row], raw.at[pl.ds(frame, frames), dst_row],
                    hs.at[i], hr.at[i], near(dtm, dh))

    down = edge(rows, 0, frames, 0, 1, 0)
    up = edge(1, rows + 1, frames, 0, -1, 1)
    down_next = edge(rows, 0, 0, 1, 1, 2)
    up_next = edge(1, rows + 1, 0, 1, -1, 3)
    along = send(raw.at[frames:, 1 : 1 + rows], raw.at[:frames, 1 : 1 + rows], hs.at[4], hr.at[4],
                 near(1, 0))
    sends = (
        (down, jnp.logical_not(bottom)),
        (up, jnp.logical_not(top)),
        (along, jnp.logical_not(last)),
        (down_next, jnp.logical_not(jnp.logical_or(bottom, last))),
        (up_next, jnp.logical_not(jnp.logical_or(top, last))),
    )
    arrivals = (
        (down, jnp.logical_not(top)),
        (up, jnp.logical_not(bottom)),
        (along, jnp.logical_not(first)),
        (down_next, jnp.logical_not(jnp.logical_or(top, first))),
        (up_next, jnp.logical_not(jnp.logical_or(bottom, first))),
    )
    for copy, there in sends:
        pl.when(there)(copy.start)

    everyone1 = send(got1, got1, s1, r1, near(1, 0))
    everyone1.wait_recv()
    here = mine[...]
    for i in range(len(peers1)):
        here = here + got1[i]
    row[...] = here
    for i, p in enumerate(peers2):
        send(row, got2.at[i], s2, r2, plane(*p)).start()

    for copy in smalls:
        copy.wait()
    weights.wait()
    for copy, there in arrivals:
        pl.when(there)(copy.wait_recv)

    everyone2 = send(got2, got2, s2, r2, near(1, 0))
    everyone2.wait_recv()
    for i in range(len(peers2)):
        here = here + got2[i]

    per_group = channels // GROUPS
    high = here.astype(jnp.bfloat16)
    rest = here - high.astype(jnp.float32)
    middle = rest.astype(jnp.bfloat16)
    low = (rest - middle.astype(jnp.float32)).astype(jnp.bfloat16)
    same = (lax.broadcasted_iota(jnp.int32, (lanes, lanes), 0) // per_group
            == lax.broadcasted_iota(jnp.int32, (lanes, lanes), 1) // per_group)
    same = jnp.where(same, 1.0, 0.0).astype(jnp.bfloat16)
    spread = sum(jnp.dot(a, same, preferred_element_type=jnp.float32) for a in (low, middle, high))
    cells = tm_n * h_n * frames * rows * cols * per_group
    spread = spread * (1.0 / cells)
    mean = spread[:parts]
    var = jnp.maximum(spread[parts:] - mean * mean, 0.0)
    scale = lax.rsqrt(var + EPSILON)

    def flat(a):
        return jnp.concatenate([a[k : k + 1] for k in range(parts)], axis=1)

    half_scale = flat(scale) * gbuf[...].reshape(1, channels) * 0.5
    half_shift = hbuf[...].reshape(1, channels) * 0.5 - flat(mean) * half_scale

    def activate(f, source, r):
        v = raw[source, r].astype(jnp.float32) * half_scale + half_shift
        act[f, r] = (v + v * jnp.tanh(v)).astype(jnp.bfloat16)

    for r in range(rows + 2):
        def line(r=r):
            for f in range(2 * frames):
                source = jnp.where(first, frames, f) if f < frames else f
                activate(f, source, r)

        def blank(r=r):
            for f in range(2 * frames):
                act[f, r] = jnp.zeros((cols, channels), jnp.bfloat16)

        if r == 0:
            pl.when(jnp.logical_not(top))(line)
            pl.when(top)(blank)
        elif r == rows + 1:
            pl.when(jnp.logical_not(bottom))(line)
            pl.when(bottom)(blank)
        else:
            line()

    offset = bbuf[...].reshape(1, 1, -1)
    m = rows * cols
    for f in range(frames):
        taps = []
        for c in range(3):
            acc = None
            for a in range(3):
                for b in range(3):
                    lhs = act[f + a, b : b + rows].reshape(m, channels)
                    part = jnp.dot(lhs, wbuf[a, b, c], preferred_element_type=jnp.float32)
                    acc = part if acc is None else acc + part
            taps.append(acc.reshape(rows, cols, -1))
        edge_zero = jnp.zeros((rows, 1, taps[0].shape[-1]), jnp.float32)
        left = jnp.concatenate([edge_zero, taps[0][:, :-1]], axis=1)
        right = jnp.concatenate([taps[2][:, 1:], edge_zero], axis=1)
        obuf[f] = (taps[1] + left + right + offset).astype(jnp.bfloat16)
    done = pltpu.make_async_copy(obuf, out, out_sem)
    done.start()
    done.wait()

    everyone1.wait_send()
    everyone2.wait_send()
    for copy, there in sends:
        pl.when(there)(copy.wait_send)


def solution(mesh):
    sizes = (mesh.shape["tm"], mesh.shape["height"])

    def on_device(features, gain, shift, weight, bias):
        frames, rows, cols, channels = features.shape
        cout = weight.shape[-1]
        n1 = 2 * sizes[1] - 1
        n2 = sizes[0] // 2 - 1
        any_space = pl.BlockSpec(memory_space=pl.ANY)
        slab = (2 * frames, rows + 2, cols, channels)
        dma = pltpu.SemaphoreType.DMA
        return pl.pallas_call(
            functools.partial(kernel, sizes),
            out_shape=jax.ShapeDtypeStruct((frames, rows, cols, cout), jnp.bfloat16),
            in_specs=[any_space] * 5,
            out_specs=any_space,
            scratch_shapes=[
                pltpu.VMEM(slab, jnp.bfloat16),
                pltpu.VMEM(slab, jnp.bfloat16),
                pltpu.VMEM(weight.shape, jnp.bfloat16),
                pltpu.VMEM((frames, rows, cols, cout), jnp.bfloat16),
                pltpu.VMEM((channels,), jnp.float32),
                pltpu.VMEM((channels,), jnp.float32),
                pltpu.VMEM((cout,), jnp.float32),
                pltpu.VMEM((8, 128), jnp.float32),
                pltpu.VMEM((8, 128), jnp.float32),
                pltpu.VMEM((n1, 8, 128), jnp.float32),
                pltpu.VMEM((n2, 8, 128), jnp.float32),
                dma, dma((3,)), dma, dma, dma, dma, dma, dma, dma((5,)), dma((5,)),
            ],
            compiler_params=pltpu.CompilerParams(
                collective_id=0, has_side_effects=True, vmem_limit_bytes=60 * 1024 * 1024
            ),
        )(features, gain, shift, weight, bias)

    return jax.shard_map(
        on_device,
        mesh=mesh,
        in_specs=(P(("clips", "tm"), "height", None, None), P(), P(), P(), P()),
        out_specs=P(("clips", "tm"), "height", None, None),
        check_vma=False,
    )
```

time: 101 us -> 43 us (0.43)
  the two profiles are of different devices: /device:TPU:528 before, /device:TPU:531 now
where the time goes in v1:
time: 43 us; the launch traced here: 42.9 us
  Pallas kernels  41.1 us (96%)
  local copies, waits for them, and re-layouts  1.77 us (4%)
    pallas_call x1, Pallas kernels, on_device(): pl.pallas_call(functools.partial(kernel, sizes), out_shape=jax.ShapeDtype...  41.1 us
    unnamed x1, local copies, waits for them, and re-layouts  1.77 us

profile of v1, /device:TPU:531, one launch (start us, length us, event | category | flops | bytes accessed | tf_op | source)
XLA Modules:
  0.0 42.9 jit_solution(12681173926596665887)
XLA Ops:
  0.0 41.1 %shard_map.55 = bf16[2,4,96,256]{3,2,1,0:T(8,128)(2,1)} custom-call(bf16[2,4,96,512]{3,2,1,0:T(8,128)(2,1)} %feat.1, f32[512]{0:T(512)} %gain.1, f32[512]{0:T(512)} %shift.1, bf16[3,3,3,512,256]{4,3,2,1,0:T(8,128)(2,1)} %weight.1, f32[256]{0:T(256)} %bias.1), custom_call_target="tpu_custom_call" | custom-call | tf_op jit(solution)/shard_map/pallas_call | solution.py:215
  41.1 1.8 %copy.7 = bf16[2,4,96,256]{3,2,1,0:T(8,128)(2,1)} copy(bf16[2,4,96,256]{3,2,1,0:T(8,128)(2,1)} %shard_map.55) | data formatting | bytes 786432

commit v2 on v1

v2 whole, which is shorter than its diff:
```python
import functools

import jax
import jax.numpy as jnp
from jax import lax
from jax.experimental import pallas as pl
from jax.experimental.pallas import tpu as pltpu
from jax.sharding import PartitionSpec as P

MESH = pl.DeviceIdType.MESH
GROUPS = 32
EPSILON = 1e-06


def kernel(sizes, feat, gain, shift, weight, bias, out, raw, act, wbuf, gbuf, hbuf, bbuf,
           mine, row, row2, late, span, got1, got2, in_sem, small_sem, w_sem, s0, r0, s1, r1, s2, r2, s4, hs, hr, perm0, perm2, perm3):
    tm_n, h_n = sizes
    y_n = tm_n // 2
    frames, rows, cols, channels = feat.shape
    lanes = 128
    parts = channels // lanes
    tm = lax.axis_index("tm")
    h = lax.axis_index("height")
    core = lax.rem(tm, 2)
    y = lax.div(tm, 2)
    first, last = tm == 0, tm == tm_n - 1
    top, bottom = h == 0, h == h_n - 1

    wide = 2 * h_n
    rank = core * h_n + h
    leader = jnp.logical_and(first, top)
    member = jnp.logical_not(leader)
    all_of, any_of, no = jnp.logical_and, jnp.logical_or, jnp.logical_not
    passes_on = any_of(all_of(core == 0, member), all_of(tm == 1, top))
    receives_along = all_of(core == 0, no(first))

    def at(dtm, dh):
        return {"tm": tm + dtm, "height": h + dh}

    def chip_row(q, frame_chip=y):
        return {"tm": frame_chip * 2 + q // h_n, "height": q % h_n}

    def column(other, c):
        return {"tm": other * 2 + c, "height": h}

    far = sorted(range(wide), key=lambda q: (-min(q % h_n, h_n - q % h_n), q))

    def when(condition, f, *args):
        pl.when(condition)(functools.partial(f, *args))

    def signal(sem, device):
        pl.semaphore_signal(sem, inc=1, device_id=device, device_id_type=MESH)

    def send(src, dst, s, r, device):
        return pltpu.make_async_remote_copy(src_ref=src, dst_ref=dst, send_sem=s, recv_sem=r,
                                            device_id=device, device_id_type=MESH)

    loads = {}
    for f in range(frames):
        for r in range(rows):
            loads[f, r] = pltpu.make_async_copy(feat.at[f, r], raw.at[frames + f, 1 + r], in_sem.at[f, r])
            loads[f, r].start()
    smalls = [pltpu.make_async_copy(a, b, small_sem.at[i])
              for i, (a, b) in enumerate(((gain, gbuf), (shift, hbuf), (bias, bbuf)))]
    for copy in smalls:
        copy.start()
    weights = pltpu.make_async_copy(weight, wbuf, w_sem)
    weights.start()

    barrier = pltpu.get_barrier_semaphore()

    @pl.when(member)
    def _():
        when(any_of(y == 0, rank == 0), signal, barrier, {"tm": 0, "height": 0})
        for q in range(wide):
            ahead = q != rank if q else all_of(rank > 0, y > 0)
            when(ahead, signal, barrier, chip_row(q))
        for other in range(1, y_n):
            when(other > y, signal, barrier, column(other, 0))
            when(other > y, signal, barrier, column(other, 1))
        when(receives_along, signal, barrier, at(-1, 0))
        when(all_of(receives_along, no(top)), signal, barrier, at(-1, -1))
        when(all_of(receives_along, no(bottom)), signal, barrier, at(-1, 1))

    total = jnp.zeros((8, channels), jnp.float32)
    squares = jnp.zeros((8, channels), jnp.float32)
    for f, r in loads:
        loads[f, r].wait()
        x = raw[frames + f, 1 + r].astype(jnp.float32).reshape(cols // 8, 8, channels)
        total = total + jnp.sum(x, axis=0)
        squares = squares + jnp.sum(x * x, axis=0)
    total = jnp.sum(total, axis=0, keepdims=True)
    squares = jnp.sum(squares, axis=0, keepdims=True)
    for k in range(parts):
        mine[k : k + 1, :] = total[:, k * lanes : (k + 1) * lanes]
        mine[parts + k : parts + k + 1, :] = squares[:, k * lanes : (k + 1) * lanes]

    def number(condition):
        return condition.astype(jnp.int32)

    beside = wide - 1 - number(y == 0)
    below = 2 * y - number(all_of(top, y > 0))
    onward = number(all_of(core == 1, no(last))) * (3 - number(top) - number(bottom))
    everybody = wide - 1 + y_n - 1
    pl.semaphore_wait(barrier, jnp.where(leader, everybody, beside + below + onward))

    def edge(src_row, dst_row, frame, dtm, dh, i):
        return send(raw.at[frames:, src_row], raw.at[pl.ds(frame, frames), dst_row],
                    hs.at[i], hr.at[i], at(dtm, dh))

    down = edge(rows, 0, frames, 0, 1, 0)
    up = edge(1, rows + 1, frames, 0, -1, 1)
    down_next = edge(rows, 0, 0, 1, 1, 2)
    up_next = edge(1, rows + 1, 0, 1, -1, 3)
    along = send(raw.at[frames:, 1 : 1 + rows], raw.at[:frames, 1 : 1 + rows], hs.at[4], hr.at[4],
                 at(1, 0))
    down_again = edge(0, 0, 0, 1, 0, 2)
    up_again = edge(rows + 1, rows + 1, 0, 1, 0, 3)
    to_leader = all_of(first, h == 1)
    sends = (
        (down, no(bottom)),
        (along, no(last)),
        (down_next, all_of(core == 1, no(any_of(bottom, last)))),
        (up_next, any_of(to_leader, all_of(core == 1, no(any_of(top, last))))),
        (up, all_of(no(top), no(to_leader))),
    )
    arrivals = (
        (down, no(top)),
        (up, no(bottom)),
        (along, no(first)),
        (down_next, no(any_of(top, first))),
        (up_next, no(any_of(bottom, first))),
    )

    def tell(device):
        return send(mine, late, s0, r0, device)

    @pl.when(leader)
    def _():
        for q in far:
            if q:
                tell(chip_row(q, 0)).start()
        signal(perm0, {"tm": 0, "height": 1})
        signal(perm0, {"tm": 1, "height": 0})

    def give(q):
        send(mine, got1.at[rank], s1.at[q], r1.at[rank], chip_row(q)).start()

    @pl.when(member)
    def _():
        for other in range(y_n - 1):
            sender = jnp.where(top, 1, 0) if other == 0 else 0
            when(other < y, signal, perm2.at[y], column(other, sender))
        when(all_of(y > 0, rank > 0), signal, perm3, column(0, core))
        for q in far:
            ahead = q != rank if q else all_of(rank > 0, y > 0)
            when(ahead, give, q)

    for copy, there in sends:
        when(there, copy.start)

    @pl.when(leader)
    def _():
        for other in range(1, y_n):
            tell(column(other, 0)).start()

    @pl.when(member)
    def _():
        got1[rank] = mine[...]

        @pl.when(y == 0)
        def _():
            got1[0] = jnp.zeros_like(mine)

        for q in range(wide):
            ahead = q != rank if q else all_of(rank > 0, y > 0)
            when(ahead, send(mine, got1.at[q], s1.at[q], r1.at[q], chip_row(q)).wait)
        here = got1[0]
        for q in range(1, wide):
            here = here + got1[q]
        row[...] = here
        got2[y] = here

        def pass_on(other, c):
            send(row, got2.at[y], s2.at[other, c], r2.at[y], column(other, c)).start()

        @pl.when(passes_on)
        def _():
            for other in range(y_n):
                @pl.when(other != y)
                def _():
                    when(other > y, pl.semaphore_wait, perm2.at[other], 2)
                    if other:
                        pass_on(other, 0)
                    else:
                        when(no(top), pass_on, other, 0)
                    pass_on(other, 1)

        @pl.when(to_leader)
        def _():
            pl.semaphore_wait(perm0, 1)
            up.start()

        for other in range(y_n):
            when(other != y, send(row, got2.at[other], s2.at[0, 0], r2.at[other], column(other, 0)).wait_recv)
        here = got2[0]
        for other in range(1, y_n):
            here = here + got2[other]
        row2[...] = here

        @pl.when(all_of(tm == 1, top))
        def _():
            pl.semaphore_wait(perm0, 1)
            send(row2, late, s0, r0, {"tm": 0, "height": 0}).start()

    @pl.when(leader)
    def _():
        row2[...] = mine[...]

    relays = all_of(member, y == 0)
    tell(at(0, 0)).wait_recv()

    @pl.when(relays)
    def _():
        pl.semaphore_wait(perm3, y_n - 1)
        for other in range(1, y_n):
            send(late, late, s4.at[other], r0, column(other, core)).start()

    for copy in smalls:
        copy.wait()
    weights.wait()
    when(no(top), down.wait_recv)
    when(all_of(core == 0, no(top)), down_again.start)
    when(no(bottom), up.wait_recv)
    when(all_of(all_of(core == 0, no(bottom)), member), up_again.start)
    for copy, there in arrivals[2:]:
        when(there, copy.wait_recv)
    here = row2[...] + late[...]

    per_group = channels // GROUPS
    high = here.astype(jnp.bfloat16)
    rest = here - high.astype(jnp.float32)
    middle = rest.astype(jnp.bfloat16)
    low = (rest - middle.astype(jnp.float32)).astype(jnp.bfloat16)
    same = (lax.broadcasted_iota(jnp.int32, (lanes, lanes), 0) // per_group
            == lax.broadcasted_iota(jnp.int32, (lanes, lanes), 1) // per_group)
    same = jnp.where(same, 1.0, 0.0).astype(jnp.bfloat16)
    spread = sum(jnp.dot(a, same, preferred_element_type=jnp.float32) for a in (low, middle, high))
    cells = tm_n * h_n * frames * rows * cols * per_group
    spread = spread * (1.0 / cells)
    mean = spread[:parts]
    var = jnp.maximum(spread[parts:] - mean * mean, 0.0)
    scale = lax.rsqrt(var + EPSILON)

    def flat(a):
        return jnp.concatenate([a[k : k + 1] for k in range(parts)], axis=1)

    half_scale = flat(scale) * gbuf[...].reshape(1, channels) * 0.5
    half_shift = hbuf[...].reshape(1, channels) * 0.5 - flat(mean) * half_scale

    def activate(f, source, r):
        v = raw[source, r].astype(jnp.float32) * half_scale + half_shift
        act[f, r] = (v + v * jnp.tanh(v)).astype(jnp.bfloat16)

    for r in range(rows + 2):
        def line(r=r):
            for f in range(2 * frames):
                source = jnp.where(first, frames, f) if f < frames else f
                activate(f, source, r)

        def blank(r=r):
            for f in range(2 * frames):
                act[f, r] = jnp.zeros((cols, channels), jnp.bfloat16)

        if r == 0:
            pl.when(jnp.logical_not(top))(line)
            pl.when(top)(blank)
        elif r == rows + 1:
            pl.when(jnp.logical_not(bottom))(line)
            pl.when(bottom)(blank)
        else:
            line()

    offset = bbuf[...].reshape(1, 1, -1)
    m = rows * cols
    for f in range(frames):
        taps = []
        for c in range(3):
            acc = None
            for a in range(3):
                for b in range(3):
                    lhs = act[f + a, b : b + rows].reshape(m, channels)
                    part = jnp.dot(lhs, wbuf[a, b, c], preferred_element_type=jnp.float32)
                    acc = part if acc is None else acc + part
            taps.append(acc.reshape(rows, cols, -1))
        edge_zero = jnp.zeros((rows, 1, taps[0].shape[-1]), jnp.float32)
        left = jnp.concatenate([edge_zero, taps[0][:, :-1]], axis=1)
        right = jnp.concatenate([taps[2][:, 1:], edge_zero], axis=1)
        out[f] = (taps[1] + left + right + offset).astype(jnp.bfloat16)
    @pl.when(leader)
    def _():
        send(span, span, s0, r0, at(0, 0)).wait_send()

    @pl.when(relays)
    def _():
        for other in range(1, y_n):
            send(late, late, s4.at[other], r0, at(0, 0)).wait_send()

    when(all_of(tm == 1, top), send(row2, late, s0, r0, at(0, 0)).wait_send)

    @pl.when(passes_on)
    def _():
        for other in range(y_n):
            for c in range(2):
                sent = other != y if other or c else all_of(other != y, no(top))
                when(sent, send(row, row, s2.at[other, c], r2.at[0], at(0, 0)).wait_send)

    for copy, there in sends[:-1]:
        when(there, copy.wait_send)
    when(no(top), up.wait_send)
    when(all_of(core == 0, no(top)), down_again.wait_send)
    when(all_of(all_of(core == 0, no(bottom)), member), up_again.wait_send)


def solution(mesh):
    sizes = (mesh.shape["tm"], mesh.shape["height"])

    def on_device(features, gain, shift, weight, bias):
        frames, rows, cols, channels = features.shape
        cout = weight.shape[-1]
        n1 = 2 * sizes[1]
        n2 = sizes[0] // 2
        any_space = pl.BlockSpec(memory_space=pl.ANY)
        slab = (2 * frames, rows + 2, cols, channels)
        dma = pltpu.SemaphoreType.DMA
        return pl.pallas_call(
            functools.partial(kernel, sizes),
            out_shape=pltpu.VMEM((frames, rows, cols, cout), jnp.bfloat16),
            in_specs=[any_space] * 5,
            out_specs=pl.BlockSpec(memory_space=pltpu.VMEM),
            scratch_shapes=[
                pltpu.VMEM(slab, jnp.bfloat16),
                pltpu.VMEM(slab, jnp.bfloat16),
                pltpu.VMEM(weight.shape, jnp.bfloat16),
                pltpu.VMEM((channels,), jnp.float32),
                pltpu.VMEM((channels,), jnp.float32),
                pltpu.VMEM((cout,), jnp.float32),
                pltpu.VMEM((8, 128), jnp.float32),
                pltpu.VMEM((8, 128), jnp.float32),
                pltpu.VMEM((8, 128), jnp.float32),
                pltpu.VMEM((8, 128), jnp.float32),
                pltpu.VMEM((n1 + n2 - 2, 8, 128), jnp.float32),
                pltpu.VMEM((n1, 8, 128), jnp.float32),
                pltpu.VMEM((n2, 8, 128), jnp.float32),
                dma((frames, rows)), dma((3,)), dma, dma, dma, dma((n1,)), dma((n1,)), dma((n2, 2)), dma((n2,)),
                dma((n2,)), dma((5,)), dma((5,)), pltpu.SemaphoreType.REGULAR, pltpu.SemaphoreType.REGULAR((n2,)),
                pltpu.SemaphoreType.REGULAR,
            ],
            compiler_params=pltpu.CompilerParams(
                collective_id=0, has_side_effects=True, vmem_limit_bytes=60 * 1024 * 1024
            ),
        )(features, gain, shift, weight, bias)

    return jax.shard_map(
        on_device,
        mesh=mesh,
        in_specs=(P(("clips", "tm"), "height", None, None), P(), P(), P(), P()),
        out_specs=P(("clips", "tm"), "height", None, None),
        check_vma=False,
    )
```

time: 43 us -> 35.1 us (0.82)
  the two profiles are of different devices: /device:TPU:531 before, /device:TPU:515 now
where the time goes in v2:
time: 35.1 us; the launch traced here: 35 us
  Pallas kernels  34.3 us (98%)
  local copies, waits for them, and re-layouts  0.75 us (2%)
    pallas_call x1, Pallas kernels, on_device(): pl.pallas_call(functools.partial(kernel, sizes), out_shape=pltpu.VMEM((fr...  34.3 us
    unnamed x1, local copies, waits for them, and re-layouts  0.75 us

profile of v2, /device:TPU:515, one launch (start us, length us, event | category | flops | bytes accessed | tf_op | source)
XLA Modules:
  0.0 35.0 jit_solution(1507730851591682303)
XLA Ops:
  0.0 34.3 %shard_map.55 = bf16[2,4,96,256]{3,2,1,0:T(8,128)(2,1)S(1)} custom-call(bf16[2,4,96,512]{3,2,1,0:T(8,128)(2,1)} %feat.1, f32[512]{0:T(512)} %gain.1, f32[512]{0:T(512)} %shift.1, bf16[3,3,3,512,256]{4,3,2,1,0:T(8,128)(2,1)} %weight.1, f32[256]{0:T(256)} %bias.1), custom_call_target="tpu_custom_call" | custom-call | tf_op jit(solution)/shard_map/pallas_call | solution.py:336
  34.3 0.7 %copy.7 = bf16[2,4,96,256]{3,2,1,0:T(8,128)(2,1)} copy(bf16[2,4,96,256]{3,2,1,0:T(8,128)(2,1)S(1)} %shard_map.55) | data formatting | bytes 786432

commit v3 on v2

--- a/solution.py
+++ b/solution.py
@@ -12,7 +12,7 @@
 EPSILON = 1e-06
 
 
-def kernel(sizes, feat, gain, shift, weight, bias, out, raw, act, wbuf, gbuf, hbuf, bbuf,
+def kernel(sizes, feat, gain, shift, weight, bias, out, raw, act, wbuf, mixed, sums, gbuf, hbuf, bbuf,
            mine, row, row2, late, span, got1, got2, in_sem, small_sem, w_sem, s0, r0, s1, r1, s2, r2, s4, hs, hr, perm0, perm2, perm3):
     tm_n, h_n = sizes
     y_n = tm_n // 2
@@ -124,6 +124,7 @@
         (up_next, any_of(to_leader, all_of(core == 1, no(any_of(top, last))))),
         (up, all_of(no(top), no(to_leader))),
     )
+    along_ends = no(first)
     arrivals = (
         (down, no(top)),
         (up, no(bottom)),
@@ -142,6 +143,12 @@
                 tell(chip_row(q, 0)).start()
         signal(perm0, {"tm": 0, "height": 1})
         signal(perm0, {"tm": 1, "height": 0})
+
+    def hand_on():
+        when(no(top), down.wait_recv)
+        when(all_of(core == 0, no(top)), down_again.start)
+        when(no(bottom), up.wait_recv)
+        when(all_of(all_of(core == 0, no(bottom)), member), up_again.start)
 
     def give(q):
         send(mine, got1.at[rank], s1.at[q], r1.at[rank], chip_row(q)).start()
@@ -196,10 +203,25 @@
                         when(no(top), pass_on, other, 0)
                     pass_on(other, 1)
 
+    weights.wait()
+
+    @pl.loop(0, 9)
+    def _(i):
+        a, c = i // 3, lax.rem(i, 3)
+        for k in range(0, channels, 64):
+            g0, g1, g2 = (wbuf[a, b, c, k : k + 64].astype(jnp.float32) for b in range(3))
+            even, odd = 0.5 * (g0 + g2), 0.5 * g1
+            mixed[a, 0, c, k : k + 64] = (even + odd).astype(jnp.bfloat16)
+            mixed[a, 1, c, k : k + 64] = (even - odd).astype(jnp.bfloat16)
+
+    @pl.when(member)
+    def _():
         @pl.when(to_leader)
         def _():
             pl.semaphore_wait(perm0, 1)
             up.start()
+
+        when(no(to_leader), hand_on)
 
         for other in range(y_n):
             when(other != y, send(row, got2.at[other], s2.at[0, 0], r2.at[other], column(other, 0)).wait_recv)
@@ -228,13 +250,7 @@
 
     for copy in smalls:
         copy.wait()
-    weights.wait()
-    when(no(top), down.wait_recv)
-    when(all_of(core == 0, no(top)), down_again.start)
-    when(no(bottom), up.wait_recv)
-    when(all_of(all_of(core == 0, no(bottom)), member), up_again.start)
-    for copy, there in arrivals[2:]:
-        when(there, copy.wait_recv)
+    when(along_ends, along.wait_recv)
     here = row2[...] + late[...]
 
     per_group = channels // GROUPS
@@ -258,45 +274,70 @@
     half_scale = flat(scale) * gbuf[...].reshape(1, channels) * 0.5
     half_shift = hbuf[...].reshape(1, channels) * 0.5 - flat(mean) * half_scale
 
-    def activate(f, source, r):
-        v = raw[source, r].astype(jnp.float32) * half_scale + half_shift
-        act[f, r] = (v + v * jnp.tanh(v)).astype(jnp.bfloat16)
-
-    for r in range(rows + 2):
-        def line(r=r):
-            for f in range(2 * frames):
-                source = jnp.where(first, frames, f) if f < frames else f
-                activate(f, source, r)
-
-        def blank(r=r):
-            for f in range(2 * frames):
-                act[f, r] = jnp.zeros((cols, channels), jnp.bfloat16)
-
-        if r == 0:
-            pl.when(jnp.logical_not(top))(line)
-            pl.when(top)(blank)
-        elif r == rows + 1:
-            pl.when(jnp.logical_not(bottom))(line)
-            pl.when(bottom)(blank)
-        else:
-            line()
-
-    offset = bbuf[...].reshape(1, 1, -1)
-    m = rows * cols
-    for f in range(frames):
-        taps = []
-        for c in range(3):
-            acc = None
-            for a in range(3):
-                for b in range(3):
-                    lhs = act[f + a, b : b + rows].reshape(m, channels)
-                    part = jnp.dot(lhs, wbuf[a, b, c], preferred_element_type=jnp.float32)
-                    acc = part if acc is None else acc + part
-            taps.append(acc.reshape(rows, cols, -1))
-        edge_zero = jnp.zeros((rows, 1, taps[0].shape[-1]), jnp.float32)
-        left = jnp.concatenate([edge_zero, taps[0][:, :-1]], axis=1)
-        right = jnp.concatenate([taps[2][:, 1:], edge_zero], axis=1)
-        out[f] = (taps[1] + left + right + offset).astype(jnp.bfloat16)
+    step = 16
+
+    def activated(f, r, k):
+        source = jnp.where(first, frames, f) if f < frames else f
+        v = raw[source, r, k : k + step].astype(jnp.float32) * half_scale + half_shift
+        return v + v * jnp.tanh(v)
+
+    def put(p, f, pair, k, value):
+        act[p, f, pair, k : k + step] = value.astype(jnp.bfloat16)
+
+    for f in range(2 * frames):
+        for k in range(0, cols, step):
+            d = [activated(f, r, k) for r in range(1, rows + 1)]
+            for pair in range(2):
+                put(1, f, pair, k, d[2 * pair] + d[2 * pair + 1])
+                put(2, f, pair, k, d[2 * pair + 1] - d[2 * pair])
+            put(0, f, 1, k, d[1] - d[3])
+            put(3, f, 0, k, d[0] - d[2])
+
+    m = frames * 2 * cols
+
+    def product(p, c):
+        acc = None
+        for a in range(3):
+            lhs = act[p, a : a + frames].reshape(m, channels)
+            rhs = wbuf[a, 2 * (p // 3), c] if p in (0, 3) else mixed[a, p - 1, c]
+            part = jnp.dot(lhs, rhs, preferred_element_type=jnp.float32)
+            acc = part if acc is None else acc + part
+        return acc
+
+    for c in range(3):
+        m1, m2 = product(1, c), product(2, c)
+        sums[c, 0] = m1 + m2
+        sums[c, 1] = m1 - m2
+
+    @pl.when(no(leader))
+    def _():
+        when(to_leader, hand_on)
+        for copy, there in arrivals[3:]:
+            when(there, copy.wait_recv)
+
+    when(leader, hand_on)
+
+    for f in range(2 * frames):
+        for k in range(0, cols, step):
+            above = jnp.where(top, 0.0, activated(f, 0, k))
+            below = jnp.where(bottom, 0.0, activated(f, rows + 1, k))
+            put(0, f, 0, k, above - activated(f, 2, k))
+            put(3, f, 1, k, activated(f, rows - 1, k) - below)
+
+    offset = bbuf[...].reshape(1, -1)
+    for c in range(3):
+        sums[c, 0] = sums[c, 0] + product(0, c)
+        sums[c, 1] = sums[c, 1] - product(3, c)
+    for odd in range(2):
+        for f in range(frames):
+            for pair in range(2):
+                at0 = (f * 2 + pair) * cols
+                left, middle, right = (sums[c, odd, at0 : at0 + cols] for c in range(3))
+                zero = jnp.zeros_like(left[:1])
+                left = jnp.concatenate([zero, left[:-1]], axis=0)
+                right = jnp.concatenate([right[1:], zero], axis=0)
+                out[f, 2 * pair + odd] = (middle + left + right + offset).astype(jnp.bfloat16)
+
     @pl.when(leader)
     def _():
         send(span, span, s0, r0, at(0, 0)).wait_send()
@@ -340,8 +381,10 @@
             out_specs=pl.BlockSpec(memory_space=pltpu.VMEM),
             scratch_shapes=[
                 pltpu.VMEM(slab, jnp.bfloat16),
-                pltpu.VMEM(slab, jnp.bfloat16),
+                pltpu.VMEM((4, 2 * frames, 2, cols, channels), jnp.bfloat16),
                 pltpu.VMEM(weight.shape, jnp.bfloat16),
+                pltpu.VMEM((3, 2, 3, channels, cout), jnp.bfloat16),
+                pltpu.VMEM((3, 2, frames * 2 * cols, cout), jnp.float32),
                 pltpu.VMEM((channels,), jnp.float32),
                 pltpu.VMEM((channels,), jnp.float32),
                 pltpu.VMEM((cout,), jnp.float32),

time: 35.1 us -> 32.2 us (0.917)
  Pallas kernels: 34.3 us -> 31.3 us
    pallas_call x1, Pallas kernels: 34.3 us -> 31.3 us  [on_device(): pl.pallas_call(functools.partial(kernel, sizes), out_shape=pltpu.VMEM((fr...]
where the time goes in v3:
time: 32.2 us; the launch traced here: 32.1 us
  Pallas kernels  31.3 us (97%)
  local copies, waits for them, and re-layouts  0.75 us (2%)
    pallas_call x1, Pallas kernels, on_device(): pl.pallas_call(functools.partial(kernel, sizes), out_shape=pltpu.VMEM((fr...  31.3 us
    unnamed x1, local copies, waits for them, and re-layouts  0.75 us

profile of v3, /device:TPU:515, one launch (start us, length us, event | category | flops | bytes accessed | tf_op | source)
XLA Modules:
  0.0 32.1 jit_solution(10578629993545605813)
XLA Ops:
  0.0 31.3 %shard_map.55 = bf16[2,4,96,256]{3,2,1,0:T(8,128)(2,1)S(1)} custom-call(bf16[2,4,96,512]{3,2,1,0:T(8,128)(2,1)} %feat.1, f32[512]{0:T(512)} %gain.1, f32[512]{0:T(512)} %shift.1, bf16[3,3,3,512,256]{4,3,2,1,0:T(8,128)(2,1)} %weight.1, f32[256]{0:T(256)} %bias.1), custom_call_target="tpu_custom_call" | custom-call | tf_op jit(solution)/shard_map/pallas_call | solution.py:377
  31.3 0.7 %copy.7 = bf16[2,4,96,256]{3,2,1,0:T(8,128)(2,1)} copy(bf16[2,4,96,256]{3,2,1,0:T(8,128)(2,1)S(1)} %shard_map.55) | data formatting | bytes 786432

commit v4 on v3

v4 whole, which is shorter than its diff:
```python
import functools

import jax
import jax.numpy as jnp
from jax import lax
from jax.experimental import pallas as pl
from jax.experimental.pallas import tpu as pltpu
from jax.sharding import PartitionSpec as P

MESH = pl.DeviceIdType.MESH
GROUPS = 32
EPSILON = 1e-06


def kernel(sizes, feat, gain, shift, weight, bias, out, raw, act, wbuf, mixed, sums, kept, gbuf, hbuf, bbuf,
           mine, pair, row, row2, late, span, got1, got2, in_sem, small_sem, w_sem, s0, r0, s1, r1, s2, r2, s4, s5, hs, hr, perm0, perm2):
    tm_n, h_n = sizes
    y_n = tm_n // 2
    frames, rows, cols, channels = feat.shape
    lanes = 128
    parts = channels // lanes
    tm = lax.axis_index("tm")
    h = lax.axis_index("height")
    core = lax.rem(tm, 2)
    y = lax.div(tm, 2)
    first, last = tm == 0, tm == tm_n - 1
    top, bottom = h == 0, h == h_n - 1

    wide = 2 * h_n
    leader = jnp.logical_and(first, top)
    member = jnp.logical_not(leader)
    all_of, any_of, no = jnp.logical_and, jnp.logical_or, jnp.logical_not
    beside_leader = all_of(tm == 1, top)
    passes_on = any_of(all_of(core == 0, member), beside_leader)
    receives_along = all_of(core == 0, no(first))
    to_leader = all_of(first, h == 1)

    def at(dtm, dh):
        return {"tm": tm + dtm, "height": h + dh}

    def in_row(other, c, chip=y):
        return {"tm": chip * 2 + c, "height": other}

    def column(other, c):
        return {"tm": other * 2 + c, "height": h}

    def turn(v):
        half = h_n // 2
        if isinstance(v, int):
            return v if v < half else half + h_n - 1 - v
        return jnp.where(v < half, v, half + h_n - 1 - v)

    here_turn = turn(h)
    def when(condition, f, *args):
        pl.when(condition)(functools.partial(f, *args))

    def signal(sem, device):
        pl.semaphore_signal(sem, inc=1, device_id=device, device_id_type=MESH)

    def send(src, dst, s, r, device):
        return pltpu.make_async_remote_copy(src_ref=src, dst_ref=dst, send_sem=s, recv_sem=r,
                                            device_id=device, device_id_type=MESH)

    loads = {}
    for f in range(frames):
        for r in range(rows):
            loads[f, r] = pltpu.make_async_copy(feat.at[f, r], raw.at[frames + f, 1 + r], in_sem.at[f, r])
            loads[f, r].start()
    smalls = [pltpu.make_async_copy(a, b, small_sem.at[i])
              for i, (a, b) in enumerate(((gain, gbuf), (shift, hbuf), (bias, bbuf)))]
    for copy in smalls:
        copy.start()
    weights = pltpu.make_async_copy(weight, wbuf, w_sem)
    weights.start()

    barrier = pltpu.get_barrier_semaphore()

    @pl.when(member)
    def _():
        for other in range(1, h_n):
            @pl.when(turn(other) > here_turn)
            def _():
                signal(barrier, in_row(other, 0))
                signal(barrier, in_row(other, 1))
        when(no(beside_leader), signal, barrier, column(y, 1 - core))
        when(no(top), signal, barrier, at(0, -1))
        when(no(bottom), signal, barrier, at(0, 1))

        @pl.when(receives_along)
        def _():
            signal(barrier, at(-1, 0))
            when(no(top), signal, barrier, at(-1, -1))
            when(no(bottom), signal, barrier, at(-1, 1))

        when(any_of(y == 0, all_of(core == 0, top)), signal, barrier, {"tm": 0, "height": 0})
        for other in range(1, y_n):
            @pl.when(other > y)
            def _():
                signal(barrier, column(other, 0))
                signal(barrier, column(other, 1))

    def number(condition):
        return condition.astype(jnp.int32)

    above_it = 2 * y - number(all_of(top, y > 0)) + 1 - number(beside_leader)
    before_it = 2 * here_turn - number(all_of(y == 0, h > 0))
    edges = number(no(bottom)) + number(no(top)) - number(to_leader)
    onward = number(all_of(core == 1, no(last))) * (3 - number(top) - number(bottom))
    for_leader = (wide - 1) + (y_n - 1) + 1
    def edge(src_row, dst_row, frame, dtm, dh, i):
        return send(raw.at[frames:, src_row], raw.at[pl.ds(frame, frames), dst_row],
                    hs.at[i], hr.at[i], at(dtm, dh))

    down = edge(rows, 0, frames, 0, 1, 0)
    up = edge(1, rows + 1, frames, 0, -1, 1)
    down_next = edge(rows, 0, 0, 1, 1, 2)
    up_next = edge(1, rows + 1, 0, 1, -1, 3)
    along = send(raw.at[frames:, 1 : 1 + rows], raw.at[:frames, 1 : 1 + rows], hs.at[4], hr.at[4],
                 at(1, 0))
    down_again = edge(0, 0, 0, 1, 0, 2)
    up_again = edge(rows + 1, rows + 1, 0, 1, 0, 3)
    down_beside = send(raw.at[:frames, rows], raw.at[:frames, 0], s5, hr.at[2], at(0, 1))
    for load in loads.values():
        load.wait()

    @pl.when(leader)
    def _():
        pl.semaphore_wait(barrier, for_leader)
        along.start()

    total = jnp.zeros((8, channels), jnp.float32)
    squares = jnp.zeros((8, channels), jnp.float32)
    for f, r in loads:
        x = raw[frames + f, 1 + r].astype(jnp.float32).reshape(cols // 8, 8, channels)
        total = total + jnp.sum(x, axis=0)
        squares = squares + jnp.sum(x * x, axis=0)
    total = jnp.sum(total, axis=0, keepdims=True)
    squares = jnp.sum(squares, axis=0, keepdims=True)
    for k in range(parts):
        mine[k : k + 1, :] = total[:, k * lanes : (k + 1) * lanes]
        mine[parts + k : parts + k + 1, :] = squares[:, k * lanes : (k + 1) * lanes]

    when(member, pl.semaphore_wait, barrier, above_it + before_it + edges + onward)

    def give(other, c):
        send(mine, got1.at[y, core], s1.at[other, c], r1.at[y, core], column(other, c)).start()

    @pl.when(member)
    def _():
        for other in range(y_n - 1):
            @pl.when(other < y)
            def _():
                if other:
                    give(other, 0)
                else:
                    when(no(top), give, other, 0)
                give(other, 1)
        when(no(beside_leader), give, y, 1 - core)

    sends = (
        (down, no(bottom)),
        (along, no(last)),
        (down_next, all_of(core == 1, no(any_of(bottom, last)))),
        (up_next, any_of(to_leader, all_of(core == 1, no(any_of(top, last))))),
        (up, all_of(no(top), no(to_leader))),
    )
    along_ends = no(first)
    arrivals = (
        (down, no(top)),
        (up, no(bottom)),
        (along, no(first)),
        (down_next, no(any_of(top, first))),
        (up_next, no(any_of(bottom, first))),
    )

    def tell(device):
        return send(mine, late, s0, r0, device)

    @pl.when(leader)
    def _():
        for q in range(h_n // 2, 0, -1):
            for c in range(2):
                tell(in_row(q, c, 0)).start()
        down.start()
        tell(in_row(0, 1, 0)).start()
        for q in range(h_n // 2 + 1, h_n):
            for c in range(2):
                tell(in_row(q, c, 0)).start()
        signal(perm0, {"tm": 0, "height": 1})
        signal(perm0, {"tm": 1, "height": 0})

    def hand_on():
        when(no(top), down.wait_recv)
        when(all_of(all_of(core == 0, no(top)), no(to_leader)), down_again.start)

    def hand_on_up():
        when(no(bottom), up.wait_recv)
        when(all_of(all_of(core == 0, no(bottom)), member), up_again.start)

    @pl.when(member)
    def _():
        for other in range(h_n):
            sender = jnp.where(y == 0, 1, 0) if other == 0 else 0
            when(turn(other) < here_turn, signal, perm2.at[h], in_row(other, sender))

    @pl.when(member)
    def _():
        for copy, there in sends:
            when(there, copy.start)

    @pl.when(leader)
    def _():
        for other in range(1, y_n):
            tell(column(other, 0)).start()

    @pl.when(member)
    def _():
        def arrived(other, c):
            send(mine, mine, s1.at[0, 0], r1.at[other, c], at(0, 0)).wait_recv()

        when(beside_leader, got1.at[0, 0].__setitem__, Ellipsis, jnp.zeros_like(mine))
        when(no(beside_leader), arrived, y, 1 - core)
        pair[...] = mine[...] + got1[y, 1 - core]
        row[...] = pair[...]
        for other in range(1, y_n):
            @pl.when(other > y)
            def _():
                arrived(other, 0)
                arrived(other, 1)
                row[...] += got1[other, 0] + got1[other, 1]

                @pl.when(passes_on)
                def _():
                    for c in range(2):
                        send(pair, got1.at[y, 0], s1.at[other, c], r1.at[y, 0], column(other, c)).start()

        for other in range(y_n):
            @pl.when(other < y)
            def _():
                arrived(other, 0)
                row[...] += got1[other, 0]

        def pass_on(other, c):
            send(row, got2.at[h], s2.at[other, c], r2.at[h], in_row(other, c)).start()

        got2[h] = row[...]

        @pl.when(passes_on)
        def _():
            for other in sorted(range(h_n), key=turn):
                @pl.when(other != h)
                def _():
                    when(turn(other) > here_turn, pl.semaphore_wait, perm2.at[other], 2)
                    if other:
                        pass_on(other, 0)
                    else:
                        when(y > 0, pass_on, other, 0)
                    pass_on(other, 1)

        when(no(to_leader), hand_on)
        hand_on_up()

    weights.wait()

    @pl.loop(0, 9)
    def _(i):
        a, c = i // 3, lax.rem(i, 3)
        for k in range(0, channels, 64):
            g0, g1, g2 = (wbuf[a, b, c, k : k + 64].astype(jnp.float32) for b in range(3))
            even, odd = 0.5 * (g0 + g2), 0.5 * g1
            mixed[a, 0, c, k : k + 64] = (even + odd).astype(jnp.bfloat16)
            mixed[a, 1, c, k : k + 64] = (even - odd).astype(jnp.bfloat16)

    @pl.when(member)
    def _():
        @pl.when(to_leader)
        def _():
            pl.semaphore_wait(perm0, 1)
            up.start()

        for other in range(h_n):
            when(other != h, send(row, got2.at[other], s2.at[0, 0], r2.at[other], at(0, 0)).wait_recv)
        here = got2[0]
        for other in range(1, h_n):
            here = here + got2[other]
        row2[...] = here

        @pl.when(beside_leader)
        def _():
            pl.semaphore_wait(perm0, 1)
            send(row2, late, s0, r0, {"tm": 0, "height": 0}).start()

    @pl.when(leader)
    def _():
        row2[...] = mine[...]

    relays = all_of(member, y == 0)
    tell(at(0, 0)).wait_recv()

    @pl.when(relays)
    def _():
        for other in range(1, y_n):
            send(late, late, s4.at[other], r0, column(other, core)).start()

    for copy in smalls:
        copy.wait()
    when(along_ends, along.wait_recv)
    when(all_of(beside_leader, no(bottom)), down_beside.start)
    when(leader, hand_on_up)
    when(arrivals[4][1], up_next.wait_recv)
    here = row2[...] + late[...]

    per_group = channels // GROUPS
    high = here.astype(jnp.bfloat16)
    rest = here - high.astype(jnp.float32)
    middle = rest.astype(jnp.bfloat16)
    low = (rest - middle.astype(jnp.float32)).astype(jnp.bfloat16)
    same = (lax.broadcasted_iota(jnp.int32, (lanes, lanes), 0) // per_group
            == lax.broadcasted_iota(jnp.int32, (lanes, lanes), 1) // per_group)
    same = jnp.where(same, 1.0, 0.0).astype(jnp.bfloat16)
    spread = sum(jnp.dot(a, same, preferred_element_type=jnp.float32) for a in (low, middle, high))
    cells = tm_n * h_n * frames * rows * cols * per_group
    spread = spread * (1.0 / cells)
    mean = spread[:parts]
    var = jnp.maximum(spread[parts:] - mean * mean, 0.0)
    scale = lax.rsqrt(var + EPSILON)

    def flat(a):
        return jnp.concatenate([a[k : k + 1] for k in range(parts)], axis=1)

    half_scale = flat(scale) * gbuf[...].reshape(1, channels) * 0.5
    half_shift = hbuf[...].reshape(1, channels) * 0.5 - flat(mean) * half_scale

    step = 16

    def activated(f, r, k):
        source = jnp.where(first, frames, f) if f < frames else f
        v = raw[source, r, k : k + step].astype(jnp.float32) * half_scale + half_shift
        return v + v * jnp.tanh(v)

    def put(p, f, pair, k, value):
        act[p, f, pair, k : k + step] = value.astype(jnp.bfloat16)

    for f in range(2 * frames):
        for k in range(0, cols, step):
            d = [activated(f, r, k) for r in range(1, rows + 1)]
            for pair in range(2):
                put(1, f, pair, k, d[2 * pair] + d[2 * pair + 1])
                put(2, f, pair, k, d[2 * pair + 1] - d[2 * pair])
            put(0, f, 1, k, d[1] - d[3])
            kept[f, k : k + step] = d[1]
            put(3, f, 0, k, d[0] - d[2])
            below = jnp.where(bottom, 0.0, activated(f, rows + 1, k))
            put(3, f, 1, k, d[2] - below)

    m = frames * 2 * cols

    def product(p, c):
        acc = None
        for a in range(3):
            lhs = act[p, a : a + frames].reshape(m, channels)
            rhs = wbuf[a, 2 * (p // 3), c] if p in (0, 3) else mixed[a, p - 1, c]
            part = jnp.dot(lhs, rhs, preferred_element_type=jnp.float32)
            acc = part if acc is None else acc + part
        return acc

    for c in range(3):
        m1, m2 = product(1, c), product(2, c)
        sums[c, 0] = m1 + m2
        sums[c, 1] = m1 - m2

    when(to_leader, hand_on)
    when(arrivals[3][1], down_next.wait_recv)

    for f in range(2 * frames):
        for k in range(0, cols, step):
            above = jnp.where(top, 0.0, activated(f, 0, k))
            put(0, f, 0, k, above - kept[f, k : k + step])

    offset = bbuf[...].reshape(1, -1)
    for c in range(3):
        sums[c, 1] = sums[c, 1] - product(3, c)
        sums[c, 0] = sums[c, 0] + product(0, c)
    for odd in range(2):
        for f in range(frames):
            for pair in range(2):
                at0 = (f * 2 + pair) * cols
                left, middle, right = (sums[c, odd, at0 : at0 + cols] for c in range(3))
                zero = jnp.zeros_like(left[:1])
                left = jnp.concatenate([zero, left[:-1]], axis=0)
                right = jnp.concatenate([right[1:], zero], axis=0)
                out[f, 2 * pair + odd] = (middle + left + right + offset).astype(jnp.bfloat16)

    @pl.when(leader)
    def _():
        send(span, span, s0, r0, at(0, 0)).wait_send()

    @pl.when(relays)
    def _():
        for other in range(1, y_n):
            send(late, late, s4.at[other], r0, at(0, 0)).wait_send()

    when(beside_leader, send(row2, late, s0, r0, at(0, 0)).wait_send)

    @pl.when(member)
    def _():
        def left(sem):
            send(mine, mine, sem, r0, at(0, 0)).wait_send()

        when(no(beside_leader), left, s1.at[y, 1 - core])
        for other in range(y_n):
            for c in range(2):
                sent = any_of(other < y, all_of(other > y, passes_on))
                if not other and not c:
                    sent = all_of(sent, no(top))
                when(sent, left, s1.at[other, c])

        @pl.when(passes_on)
        def _():
            for other in range(h_n):
                for c in range(2):
                    sent = other != h if other or c else all_of(other != h, y > 0)
                    when(sent, left, s2.at[other, c])

    for copy, there in sends[:-1]:
        when(there, copy.wait_send)
    when(no(top), up.wait_send)
    when(all_of(all_of(core == 0, no(top)), no(to_leader)), down_again.wait_send)
    when(all_of(beside_leader, no(bottom)), down_beside.wait_send)
    when(all_of(all_of(core == 0, no(bottom)), member), up_again.wait_send)


def solution(mesh):
    sizes = (mesh.shape["tm"], mesh.shape["height"])

    def on_device(features, gain, shift, weight, bias):
        frames, rows, cols, channels = features.shape
        cout = weight.shape[-1]
        y_n, h_n = sizes[0] // 2, sizes[1]
        any_space = pl.BlockSpec(memory_space=pl.ANY)
        slab = (2 * frames, rows + 2, cols, channels)
        dma = pltpu.SemaphoreType.DMA
        return pl.pallas_call(
            functools.partial(kernel, sizes),
            out_shape=pltpu.VMEM((frames, rows, cols, cout), jnp.bfloat16),
            in_specs=[any_space] * 5,
            out_specs=pl.BlockSpec(memory_space=pltpu.VMEM),
            scratch_shapes=[
                pltpu.VMEM(slab, jnp.bfloat16),
                pltpu.VMEM((4, 2 * frames, 2, cols, channels), jnp.bfloat16),
                pltpu.VMEM(weight.shape, jnp.bfloat16),
                pltpu.VMEM((3, 2, 3, channels, cout), jnp.bfloat16),
                pltpu.VMEM((3, 2, frames * 2 * cols, cout), jnp.float32),
                pltpu.VMEM((2 * frames, cols, channels), jnp.float32),
                pltpu.VMEM((channels,), jnp.float32),
                pltpu.VMEM((channels,), jnp.float32),
                pltpu.VMEM((cout,), jnp.float32),
                *[pltpu.VMEM((8, 128), jnp.float32)] * 5,
                pltpu.VMEM((2 * h_n - 1 + y_n - 1, 8, 128), jnp.float32),
                pltpu.VMEM((y_n, 2, 8, 128), jnp.float32),
                pltpu.VMEM((h_n, 8, 128), jnp.float32),
                dma((frames, rows)), dma((3,)), dma, dma, dma, dma((y_n, 2)), dma((y_n, 2)),
                dma((h_n, 2)), dma((h_n,)), dma((y_n,)), dma, dma((5,)), dma((5,)),
                pltpu.SemaphoreType.REGULAR, pltpu.SemaphoreType.REGULAR((h_n,)),
            ],
            compiler_params=pltpu.CompilerParams(
                collective_id=0, has_side_effects=True, vmem_limit_bytes=60 * 1024 * 1024
            ),
        )(features, gain, shift, weight, bias)

    return jax.shard_map(
        on_device,
        mesh=mesh,
        in_specs=(P(("clips", "tm"), "height", None, None), P(), P(), P(), P()),
        out_specs=P(("clips", "tm"), "height", None, None),
        check_vma=False,
    )
```

time: 32.2 us -> 30.7 us (0.953)
  Pallas kernels: 31.3 us -> 29.8 us
    pallas_call x1, Pallas kernels: 31.3 us -> 29.8 us  [on_device(): pl.pallas_call(functools.partial(kernel, sizes), out_shape=pltpu.VMEM((fr...]
where the time goes in v4:
time: 30.7 us; the launch traced here: 30.6 us
  Pallas kernels  29.8 us (97%)
  local copies, waits for them, and re-layouts  0.75 us (2%)
    pallas_call x1, Pallas kernels, on_device(): pl.pallas_call(functools.partial(kernel, sizes), out_shape=pltpu.VMEM((fr...  29.8 us
    unnamed x1, local copies, waits for them, and re-layouts  0.75 us

profile of v4, /device:TPU:515, one launch (start us, length us, event | category | flops | bytes accessed | tf_op | source)
XLA Modules:
  0.0 30.6 jit_solution(11831775063644898264)
XLA Ops:
  0.0 29.8 %shard_map.55 = bf16[2,4,96,256]{3,2,1,0:T(8,128)(2,1)S(1)} custom-call(bf16[2,4,96,512]{3,2,1,0:T(8,128)(2,1)} %feat.1, f32[512]{0:T(512)} %gain.1, f32[512]{0:T(512)} %shift.1, bf16[3,3,3,512,256]{4,3,2,1,0:T(8,128)(2,1)} %weight.1, f32[256]{0:T(256)} %bias.1), custom_call_target="tpu_custom_call" | custom-call | tf_op jit(solution)/shard_map/pallas_call | solution.py:443
  29.9 0.7 %copy.7 = bf16[2,4,96,256]{3,2,1,0:T(8,128)(2,1)} copy(bf16[2,4,96,256]{3,2,1,0:T(8,128)(2,1)S(1)} %shard_map.55) | data formatting | bytes 786432

commit v5 on v4

--- a/solution.py
+++ b/solution.py
@@ -17,50 +17,6 @@
     tm_n, h_n = sizes
     y_n = tm_n // 2
     frames, rows, cols, channels = feat.shape
-    lanes = 128
-    parts = channels // lanes
-    tm = lax.axis_index("tm")
-    h = lax.axis_index("height")
-    core = lax.rem(tm, 2)
-    y = lax.div(tm, 2)
-    first, last = tm == 0, tm == tm_n - 1
-    top, bottom = h == 0, h == h_n - 1
-
-    wide = 2 * h_n
-    leader = jnp.logical_and(first, top)
-    member = jnp.logical_not(leader)
-    all_of, any_of, no = jnp.logical_and, jnp.logical_or, jnp.logical_not
-    beside_leader = all_of(tm == 1, top)
-    passes_on = any_of(all_of(core == 0, member), beside_leader)
-    receives_along = all_of(core == 0, no(first))
-    to_leader = all_of(first, h == 1)
-
-    def at(dtm, dh):
-        return {"tm": tm + dtm, "height": h + dh}
-
-    def in_row(other, c, chip=y):
-        return {"tm": chip * 2 + c, "height": other}
-
-    def column(other, c):
-        return {"tm": other * 2 + c, "height": h}
-
-    def turn(v):
-        half = h_n // 2
-        if isinstance(v, int):
-            return v if v < half else half + h_n - 1 - v
-        return jnp.where(v < half, v, half + h_n - 1 - v)
-
-    here_turn = turn(h)
-    def when(condition, f, *args):
-        pl.when(condition)(functools.partial(f, *args))
-
-    def signal(sem, device):
-        pl.semaphore_signal(sem, inc=1, device_id=device, device_id_type=MESH)
-
-    def send(src, dst, s, r, device):
-        return pltpu.make_async_remote_copy(src_ref=src, dst_ref=dst, send_sem=s, recv_sem=r,
-                                            device_id=device, device_id_type=MESH)
-
     loads = {}
     for f in range(frames):
         for r in range(rows):
@@ -71,13 +27,57 @@
     for copy in smalls:
         copy.start()
     weights = pltpu.make_async_copy(weight, wbuf, w_sem)
-    weights.start()
+
+    lanes = 128
+    parts = channels // lanes
+    tm = lax.axis_index("tm")
+    h = lax.axis_index("height")
+    core = lax.rem(tm, 2)
+    y = lax.div(tm, 2)
+    first, last = tm == 0, tm == tm_n - 1
+    top, bottom = h == 0, h == h_n - 1
+
+    wide = 2 * h_n
+    leader = jnp.logical_and(first, top)
+    member = jnp.logical_not(leader)
+    all_of, any_of, no = jnp.logical_and, jnp.logical_or, jnp.logical_not
+    beside_leader = all_of(tm == 1, top)
+    passes_on = any_of(all_of(core == 0, member), beside_leader)
+    receives_along = all_of(core == 0, no(first))
+    relays = all_of(core == 1, y == 0)
+    to_leader = all_of(first, h == 1)
+
+    def at(dtm, dh):
+        return {"tm": tm + dtm, "height": h + dh}
+
+    def in_row(other, c, chip=y):
+        return {"tm": chip * 2 + c, "height": other}
+
+    def column(other, c):
+        return {"tm": other * 2 + c, "height": h}
+
+    def turn(v):
+        half = h_n // 2
+        if isinstance(v, int):
+            return v if v < half else half + h_n - 1 - v
+        return jnp.where(v < half, v, half + h_n - 1 - v)
+
+    here_turn = turn(h)
+    def when(condition, f, *args):
+        pl.when(condition)(functools.partial(f, *args))
+
+    def signal(sem, device):
+        pl.semaphore_signal(sem, inc=1, device_id=device, device_id_type=MESH)
+
+    def send(src, dst, s, r, device):
+        return pltpu.make_async_remote_copy(src_ref=src, dst_ref=dst, send_sem=s, recv_sem=r,
+                                            device_id=device, device_id_type=MESH)
 
     barrier = pltpu.get_barrier_semaphore()
 
     @pl.when(member)
     def _():
-        for other in range(1, h_n):
+        for other in sorted(range(1, h_n), key=lambda q: -turn(q)):
             @pl.when(turn(other) > here_turn)
             def _():
                 signal(barrier, in_row(other, 0))
@@ -120,27 +120,21 @@
     down_again = edge(0, 0, 0, 1, 0, 2)
     up_again = edge(rows + 1, rows + 1, 0, 1, 0, 3)
     down_beside = send(raw.at[:frames, rows], raw.at[:frames, 0], s5, hr.at[2], at(0, 1))
-    for load in loads.values():
-        load.wait()
-
-    @pl.when(leader)
-    def _():
-        pl.semaphore_wait(barrier, for_leader)
-        along.start()
-
     total = jnp.zeros((8, channels), jnp.float32)
     squares = jnp.zeros((8, channels), jnp.float32)
     for f, r in loads:
+        loads[f, r].wait()
         x = raw[frames + f, 1 + r].astype(jnp.float32).reshape(cols // 8, 8, channels)
         total = total + jnp.sum(x, axis=0)
         squares = squares + jnp.sum(x * x, axis=0)
+    weights.start()
     total = jnp.sum(total, axis=0, keepdims=True)
     squares = jnp.sum(squares, axis=0, keepdims=True)
     for k in range(parts):
         mine[k : k + 1, :] = total[:, k * lanes : (k + 1) * lanes]
         mine[parts + k : parts + k + 1, :] = squares[:, k * lanes : (k + 1) * lanes]
 
-    when(member, pl.semaphore_wait, barrier, above_it + before_it + edges + onward)
+    pl.semaphore_wait(barrier, jnp.where(leader, for_leader, above_it + before_it + edges + onward))
 
     def give(other, c):
         send(mine, got1.at[y, core], s1.at[other, c], r1.at[y, core], column(other, c)).start()
@@ -164,7 +158,7 @@
         (up_next, any_of(to_leader, all_of(core == 1, no(any_of(top, last))))),
         (up, all_of(no(top), no(to_leader))),
     )
-    along_ends = no(first)
+    along_ends = all_of(no(first), any_of(no(beside_leader), bottom))
     arrivals = (
         (down, no(top)),
         (up, no(bottom)),
@@ -178,14 +172,12 @@
 
     @pl.when(leader)
     def _():
-        for q in range(h_n // 2, 0, -1):
+        for q in sorted(range(h_n), key=lambda q: -min(q, h_n - q)):
             for c in range(2):
-                tell(in_row(q, c, 0)).start()
+                if q or c:
+                    tell(in_row(q, c, 0)).start()
+        along.start()
         down.start()
-        tell(in_row(0, 1, 0)).start()
-        for q in range(h_n // 2 + 1, h_n):
-            for c in range(2):
-                tell(in_row(q, c, 0)).start()
         signal(perm0, {"tm": 0, "height": 1})
         signal(perm0, {"tm": 1, "height": 0})
 
@@ -200,8 +192,7 @@
     @pl.when(member)
     def _():
         for other in range(h_n):
-            sender = jnp.where(y == 0, 1, 0) if other == 0 else 0
-            when(turn(other) < here_turn, signal, perm2.at[h], in_row(other, sender))
+            when(turn(other) < here_turn, signal, perm2.at[h], in_row(other, 1))
 
     @pl.when(member)
     def _():
@@ -245,7 +236,7 @@
 
         got2[h] = row[...]
 
-        @pl.when(passes_on)
+        @pl.when(core == 1)
         def _():
             for other in sorted(range(h_n), key=turn):
                 @pl.when(other != h)
@@ -278,6 +269,18 @@
             pl.semaphore_wait(perm0, 1)
             up.start()
 
+        @pl.when(all_of(beside_leader, no(bottom)))
+        def _():
+            along.wait_recv()
+            down_beside.start()
+
+        @pl.when(relays)
+        def _():
+            tell(at(0, 0)).wait_recv()
+            for other in range(1, y_n):
+                when(no(top), send(late, late, s4.at[other, 0], r0, column(other, 0)).start)
+                send(late, late, s4.at[other, 1], r0, column(other, 1)).start()
+
         for other in range(h_n):
             when(other != h, send(row, got2.at[other], s2.at[0, 0], r2.at[other], at(0, 0)).wait_recv)
         here = got2[0]
@@ -294,18 +297,11 @@
     def _():
         row2[...] = mine[...]
 
-    relays = all_of(member, y == 0)
-    tell(at(0, 0)).wait_recv()
-
-    @pl.when(relays)
-    def _():
-        for other in range(1, y_n):
-            send(late, late, s4.at[other], r0, column(other, core)).start()
+    when(no(relays), tell(at(0, 0)).wait_recv)
 
     for copy in smalls:
         copy.wait()
     when(along_ends, along.wait_recv)
-    when(all_of(beside_leader, no(bottom)), down_beside.start)
     when(leader, hand_on_up)
     when(arrivals[4][1], up_next.wait_recv)
     here = row2[...] + late[...]
@@ -398,7 +394,8 @@
     @pl.when(relays)
     def _():
         for other in range(1, y_n):
-            send(late, late, s4.at[other], r0, at(0, 0)).wait_send()
+            when(no(top), send(late, late, s4.at[other, 0], r0, at(0, 0)).wait_send)
+            send(late, late, s4.at[other, 1], r0, at(0, 0)).wait_send()
 
     when(beside_leader, send(row2, late, s0, r0, at(0, 0)).wait_send)
 
@@ -415,7 +412,7 @@
                     sent = all_of(sent, no(top))
                 when(sent, left, s1.at[other, c])
 
-        @pl.when(passes_on)
+        @pl.when(core == 1)
         def _():
             for other in range(h_n):
                 for c in range(2):
@@ -460,7 +457,7 @@
                 pltpu.VMEM((y_n, 2, 8, 128), jnp.float32),
                 pltpu.VMEM((h_n, 8, 128), jnp.float32),
                 dma((frames, rows)), dma((3,)), dma, dma, dma, dma((y_n, 2)), dma((y_n, 2)),
-                dma((h_n, 2)), dma((h_n,)), dma((y_n,)), dma, dma((5,)), dma((5,)),
+                dma((h_n, 2)), dma((h_n,)), dma((y_n, 2)), dma, dma((7,)), dma((7,)),
                 pltpu.SemaphoreType.REGULAR, pltpu.SemaphoreType.REGULAR((h_n,)),
             ],
             compiler_params=pltpu.CompilerParams(

time: 30.7 us -> 30.8 us (level)
  no operation moved by 1% of the time
where the time goes in v5:
time: 30.8 us; the launch traced here: 30.6 us
  Pallas kernels  29.8 us (97%)
  local copies, waits for them, and re-layouts  0.75 us (2%)
    pallas_call x1, Pallas kernels, on_device(): pl.pallas_call(functools.partial(kernel, sizes), out_shape=pltpu.VMEM((fr...  29.8 us
    unnamed x1, local copies, waits for them, and re-layouts  0.75 us

profile of v5, /device:TPU:515, one launch (start us, length us, event | category | flops | bytes accessed | tf_op | source)
XLA Modules:
  0.0 30.6 jit_solution(18319550176450333702)
XLA Ops:
  0.0 29.8 %shard_map.55 = bf16[2,4,96,256]{3,2,1,0:T(8,128)(2,1)S(1)} custom-call(bf16[2,4,96,512]{3,2,1,0:T(8,128)(2,1)} %feat.1, f32[512]{0:T(512)} %gain.1, f32[512]{0:T(512)} %shift.1, bf16[3,3,3,512,256]{4,3,2,1,0:T(8,128)(2,1)} %weight.1, f32[256]{0:T(256)} %bias.1), custom_call_target="tpu_custom_call" | custom-call | tf_op jit(solution)/shard_map/pallas_call | solution.py:440
  29.9 0.7 %copy.7 = bf16[2,4,96,256]{3,2,1,0:T(8,128)(2,1)} copy(bf16[2,4,96,256]{3,2,1,0:T(8,128)(2,1)S(1)} %shard_map.55) | data formatting | bytes 786432

commit v6 on v5

--- a/solution.py
+++ b/solution.py
@@ -44,7 +44,6 @@
     beside_leader = all_of(tm == 1, top)
     passes_on = any_of(all_of(core == 0, member), beside_leader)
     receives_along = all_of(core == 0, no(first))
-    relays = all_of(core == 1, y == 0)
     to_leader = all_of(first, h == 1)
 
     def at(dtm, dh):
@@ -77,7 +76,7 @@
 
     @pl.when(member)
     def _():
-        for other in sorted(range(1, h_n), key=lambda q: -turn(q)):
+        for other in range(1, h_n):
             @pl.when(turn(other) > here_turn)
             def _():
                 signal(barrier, in_row(other, 0))
@@ -192,7 +191,8 @@
     @pl.when(member)
     def _():
         for other in range(h_n):
-            when(turn(other) < here_turn, signal, perm2.at[h], in_row(other, 1))
+            sender = jnp.where(y == 0, 1, 0) if other == 0 else 0
+            when(turn(other) < here_turn, signal, perm2.at[h], in_row(other, sender))
 
     @pl.when(member)
     def _():
@@ -236,7 +236,7 @@
 
         got2[h] = row[...]
 
-        @pl.when(core == 1)
+        @pl.when(passes_on)
         def _():
             for other in sorted(range(h_n), key=turn):
                 @pl.when(other != h)
@@ -274,13 +274,6 @@
             along.wait_recv()
             down_beside.start()
 
-        @pl.when(relays)
-        def _():
-            tell(at(0, 0)).wait_recv()
-            for other in range(1, y_n):
-                when(no(top), send(late, late, s4.at[other, 0], r0, column(other, 0)).start)
-                send(late, late, s4.at[other, 1], r0, column(other, 1)).start()
-
         for other in range(h_n):
             when(other != h, send(row, got2.at[other], s2.at[0, 0], r2.at[other], at(0, 0)).wait_recv)
         here = got2[0]
@@ -297,7 +290,13 @@
     def _():
         row2[...] = mine[...]
 
-    when(no(relays), tell(at(0, 0)).wait_recv)
+    relays = all_of(member, y == 0)
+    tell(at(0, 0)).wait_recv()
+
+    @pl.when(relays)
+    def _():
+        for other in range(1, y_n):
+            send(late, late, s4.at[other], r0, column(other, core)).start()
 
     for copy in smalls:
         copy.wait()
@@ -394,8 +393,7 @@
     @pl.when(relays)
     def _():
         for other in range(1, y_n):
-            when(no(top), send(late, late, s4.at[other, 0], r0, at(0, 0)).wait_send)
-            send(late, late, s4.at[other, 1], r0, at(0, 0)).wait_send()
+            send(late, late, s4.at[other], r0, at(0, 0)).wait_send()
 
     when(beside_leader, send(row2, late, s0, r0, at(0, 0)).wait_send)
 
@@ -412,7 +410,7 @@
                     sent = all_of(sent, no(top))
                 when(sent, left, s1.at[other, c])
 
-        @pl.when(core == 1)
+        @pl.when(passes_on)
         def _():
             for other in range(h_n):
                 for c in range(2):
@@ -457,7 +455,7 @@
                 pltpu.VMEM((y_n, 2, 8, 128), jnp.float32),
                 pltpu.VMEM((h_n, 8, 128), jnp.float32),
                 dma((frames, rows)), dma((3,)), dma, dma, dma, dma((y_n, 2)), dma((y_n, 2)),
-                dma((h_n, 2)), dma((h_n,)), dma((y_n, 2)), dma, dma((7,)), dma((7,)),
+                dma((h_n, 2)), dma((h_n,)), dma((y_n,)), dma, dma((5,)), dma((5,)),
                 pltpu.SemaphoreType.REGULAR, pltpu.SemaphoreType.REGULAR((h_n,)),
             ],
             compiler_params=pltpu.CompilerParams(

time: 30.8 us -> 30.7 us (level)
  no operation moved by 1% of the time
where the time goes in v6:
time: 30.7 us; the launch traced here: 30.5 us
  Pallas kernels  29.7 us (97%)
  local copies, waits for them, and re-layouts  0.75 us (2%)
    pallas_call x1, Pallas kernels, on_device(): pl.pallas_call(functools.partial(kernel, sizes), out_shape=pltpu.VMEM((fr...  29.7 us
    unnamed x1, local copies, waits for them, and re-layouts  0.75 us

profile of v6, /device:TPU:515, one launch (start us, length us, event | category | flops | bytes accessed | tf_op | source)
XLA Modules:
  0.0 30.5 jit_solution(17560740693398744559)
XLA Ops:
  0.0 29.7 %shard_map.55 = bf16[2,4,96,256]{3,2,1,0:T(8,128)(2,1)S(1)} custom-call(bf16[2,4,96,512]{3,2,1,0:T(8,128)(2,1)} %feat.1, f32[512]{0:T(512)} %gain.1, f32[512]{0:T(512)} %shift.1, bf16[3,3,3,512,256]{4,3,2,1,0:T(8,128)(2,1)} %weight.1, f32[256]{0:T(256)} %bias.1), custom_call_target="tpu_custom_call" | custom-call | tf_op jit(solution)/shard_map/pallas_call | solution.py:438
  29.7 0.7 %copy.7 = bf16[2,4,96,256]{3,2,1,0:T(8,128)(2,1)} copy(bf16[2,4,96,256]{3,2,1,0:T(8,128)(2,1)S(1)} %shard_map.55) | data formatting | bytes 786432

commit v7 on v6

--- a/solution.py
+++ b/solution.py
@@ -114,8 +114,8 @@
     up = edge(1, rows + 1, frames, 0, -1, 1)
     down_next = edge(rows, 0, 0, 1, 1, 2)
     up_next = edge(1, rows + 1, 0, 1, -1, 3)
-    along = send(raw.at[frames:, 1 : 1 + rows], raw.at[:frames, 1 : 1 + rows], hs.at[4], hr.at[4],
-                 at(1, 0))
+    along = send(raw.at[frames:, 1:rows], raw.at[:frames, 1:rows], hs.at[4], hr.at[4], at(1, 0))
+    along_edge = send(raw.at[frames:, rows], raw.at[:frames, rows], hs.at[5], hr.at[5], at(1, 0))
     down_again = edge(0, 0, 0, 1, 0, 2)
     up_again = edge(rows + 1, rows + 1, 0, 1, 0, 3)
     down_beside = send(raw.at[:frames, rows], raw.at[:frames, 0], s5, hr.at[2], at(0, 1))
@@ -152,6 +152,7 @@
 
     sends = (
         (down, no(bottom)),
+        (along_edge, no(last)),
         (along, no(last)),
         (down_next, all_of(core == 1, no(any_of(bottom, last)))),
         (up_next, any_of(to_leader, all_of(core == 1, no(any_of(top, last))))),
@@ -175,6 +176,7 @@
             for c in range(2):
                 if q or c:
                     tell(in_row(q, c, 0)).start()
+        along_edge.start()
         along.start()
         down.start()
         signal(perm0, {"tm": 0, "height": 1})
@@ -271,7 +273,7 @@
 
         @pl.when(all_of(beside_leader, no(bottom)))
         def _():
-            along.wait_recv()
+            along_edge.wait_recv()
             down_beside.start()
 
         for other in range(h_n):
@@ -300,7 +302,6 @@
 
     for copy in smalls:
         copy.wait()
-    when(along_ends, along.wait_recv)
     when(leader, hand_on_up)
     when(arrivals[4][1], up_next.wait_recv)
     here = row2[...] + late[...]
@@ -336,7 +337,7 @@
     def put(p, f, pair, k, value):
         act[p, f, pair, k : k + step] = value.astype(jnp.bfloat16)
 
-    for f in range(2 * frames):
+    def prepare(f):
         for k in range(0, cols, step):
             d = [activated(f, r, k) for r in range(1, rows + 1)]
             for pair in range(2):
@@ -348,11 +349,14 @@
             below = jnp.where(bottom, 0.0, activated(f, rows + 1, k))
             put(3, f, 1, k, d[2] - below)
 
+    for f in range(frames, 2 * frames):
+        prepare(f)
+
     m = frames * 2 * cols
 
-    def product(p, c):
+    def product(p, c, taps=(0, 1, 2)):
         acc = None
-        for a in range(3):
+        for a in taps:
             lhs = act[p, a : a + frames].reshape(m, channels)
             rhs = wbuf[a, 2 * (p // 3), c] if p in (0, 3) else mixed[a, p - 1, c]
             part = jnp.dot(lhs, rhs, preferred_element_type=jnp.float32)
@@ -360,9 +364,18 @@
         return acc
 
     for c in range(3):
-        m1, m2 = product(1, c), product(2, c)
+        m1, m2 = product(1, c, (2,)), product(2, c, (2,))
         sums[c, 0] = m1 + m2
         sums[c, 1] = m1 - m2
+
+    when(no(first), along.wait_recv)
+    when(along_ends, along_edge.wait_recv)
+    for f in range(frames):
+        prepare(f)
+    for c in range(3):
+        m1, m2 = product(1, c, (0, 1)), product(2, c, (0, 1))
+        sums[c, 0] = sums[c, 0] + (m1 + m2)
+        sums[c, 1] = sums[c, 1] + (m1 - m2)
 
     when(to_leader, hand_on)
     when(arrivals[3][1], down_next.wait_recv)
@@ -455,7 +468,7 @@
                 pltpu.VMEM((y_n, 2, 8, 128), jnp.float32),
                 pltpu.VMEM((h_n, 8, 128), jnp.float32),
                 dma((frames, rows)), dma((3,)), dma, dma, dma, dma((y_n, 2)), dma((y_n, 2)),
-                dma((h_n, 2)), dma((h_n,)), dma((y_n,)), dma, dma((5,)), dma((5,)),
+                dma((h_n, 2)), dma((h_n,)), dma((y_n,)), dma, dma((6,)), dma((6,)),
                 pltpu.SemaphoreType.REGULAR, pltpu.SemaphoreType.REGULAR((h_n,)),
             ],
             compiler_params=pltpu.CompilerParams(

time: 30.7 us -> 30.7 us (level)
  no operation moved by 1% of the time
where the time goes in v7:
time: 30.7 us; the launch traced here: 30.5 us
  Pallas kernels  29.7 us (97%)
  local copies, waits for them, and re-layouts  0.75 us (2%)
    pallas_call x1, Pallas kernels, on_device(): pl.pallas_call(functools.partial(kernel, sizes), out_shape=pltpu.VMEM((fr...  29.7 us
    unnamed x1, local copies, waits for them, and re-layouts  0.75 us

profile of v7, /device:TPU:515, one launch (start us, length us, event | category | flops | bytes accessed | tf_op | source)
XLA Modules:
  0.0 30.5 jit_solution(13071982101988892996)
XLA Ops:
  0.0 29.7 %shard_map.55 = bf16[2,4,96,256]{3,2,1,0:T(8,128)(2,1)S(1)} custom-call(bf16[2,4,96,512]{3,2,1,0:T(8,128)(2,1)} %feat.1, f32[512]{0:T(512)} %gain.1, f32[512]{0:T(512)} %shift.1, bf16[3,3,3,512,256]{4,3,2,1,0:T(8,128)(2,1)} %weight.1, f32[256]{0:T(256)} %bias.1), custom_call_target="tpu_custom_call" | custom-call | tf_op jit(solution)/shard_map/pallas_call | solution.py:451
  29.8 0.7 %copy.7 = bf16[2,4,96,256]{3,2,1,0:T(8,128)(2,1)} copy(bf16[2,4,96,256]{3,2,1,0:T(8,128)(2,1)S(1)} %shard_map.55) | data formatting | bytes 786432
